TPU v7x, 128 devices: a whole 4x4x4 slice. The times are simulated.
128 devices in a mesh: dp: 1, ctx: 128 (over z, y, x, core).
Axes of the slice: x: 4, y: 4, z: 4, core: 2. Of those that a mesh axis runs over, the one named last changes fastest.
Arguments:
- q_seq: bfloat16 [1, 32768, 4, 128], P('dp', 'ctx')
- k_seq: bfloat16 [1, 32768, 1, 128], P('dp', 'ctx')
- v_seq: bfloat16 [1, 32768, 1, 128], P('dp', 'ctx')
- do_seq: bfloat16 [1, 32768, 4, 128], P('dp', 'ctx')
Outputs:
- output 1: bfloat16 [1, 32768, 4, 128], P('dp', 'ctx')
- output 2: bfloat16 [1, 32768, 4, 128], P('dp', 'ctx')
- output 3: bfloat16 [1, 32768, 1, 128], P('dp', 'ctx')
- output 4: bfloat16 [1, 32768, 1, 128], P('dp', 'ctx')
All inputs are finite; a program needn't handle non-finite values.
Results may differ from a plain program's by a relative error of at most 0.00819087.
Values are sent between devices in bfloat16 or wider.
A program may use at most 1 GiB of HBM per device.

v0:
```python
import jax
import jax.numpy as jnp
from jax import lax
from jax.sharding import PartitionSpec as P

WINDOW = 4096
NEG_BIG = -1e30


def fwd_update(state, q_five, k_blk, v_blk, keep_mask, sm_scale):
    m_run, l_run, o_acc = state
    scores = jnp.einsum('bqhgd,bkhd->bhgqk', q_five, k_blk, preferred_element_type=jnp.float32) * sm_scale
    scores = jnp.where(keep_mask, scores, NEG_BIG)
    m_new = jnp.maximum(m_run, jnp.max(scores, axis=-1))
    rescale = jnp.exp(m_run - m_new)
    p_blk = jnp.exp(scores - m_new[..., None])
    l_new = rescale * l_run + jnp.sum(p_blk, axis=-1)
    pv_blk = jnp.einsum('bhgqk,bkhd->bhgqd', p_blk.astype(jnp.bfloat16), v_blk, preferred_element_type=jnp.float32)
    return m_new, l_new, rescale[..., None] * o_acc + pv_blk


def bwd_block(q_five, do_five, log_sum, d_row, k_blk, v_blk, keep_mask, sm_scale):
    scores = jnp.einsum('bqhgd,bkhd->bhgqk', q_five, k_blk, preferred_element_type=jnp.float32) * sm_scale
    p_blk = jnp.exp(jnp.where(keep_mask, scores, NEG_BIG) - log_sum[..., None])
    d_prob = jnp.einsum('bqhgd,bkhd->bhgqk', do_five, v_blk, preferred_element_type=jnp.float32)
    d_score = (p_blk * (d_prob - d_row[..., None])).astype(jnp.bfloat16)
    dv_part = jnp.einsum('bhgqk,bqhgd->bkhd', p_blk.astype(jnp.bfloat16), do_five, preferred_element_type=jnp.float32)
    dq_part = jnp.einsum('bhgqk,bkhd->bqhgd', d_score, k_blk, preferred_element_type=jnp.float32) * sm_scale
    dk_part = jnp.einsum('bhgqk,bqhgd->bkhd', d_score, q_five, preferred_element_type=jnp.float32) * sm_scale
    return dq_part, dk_part, dv_part


def solution(mesh):
    n_ctx = mesh.shape['ctx']
    seq_spec = P('dp', 'ctx', None, None)
    shift_perm = [(j, (j + 1) % n_ctx) for j in range(n_ctx)]

    def local_attn(q_loc, k_loc, v_loc, do_loc):
        n_batch, chunk_len, q_heads, head_dim = q_loc.shape
        kv_heads = k_loc.shape[2]
        q_group = q_heads // kv_heads
        n_blocks = WINDOW // chunk_len
        sm_scale = head_dim ** -0.5
        dev_idx = lax.axis_index('ctx')
        five_shape = (n_batch, chunk_len, kv_heads, q_group, head_dim)
        q_five = q_loc.reshape(five_shape)
        do_five = do_loc.reshape(five_shape)
        offsets = jnp.arange(chunk_len)[:, None] - jnp.arange(chunk_len)[None, :]

        def block_mask(step_id):
            dist = step_id * chunk_len + offsets
            return (dist >= 0) & (dist < WINDOW) & (dev_idx >= step_id)

        stat_shape = (n_batch, kv_heads, q_group, chunk_len)
        init = (jnp.full(stat_shape, NEG_BIG, jnp.float32), jnp.zeros(stat_shape, jnp.float32), jnp.zeros(stat_shape + (head_dim,), jnp.float32))
        state = fwd_update(init, q_five, k_loc, v_loc, block_mask(0), sm_scale)

        def fwd_body(step_id, carry):
            kv_blk, run_state = carry
            kv_blk = lax.ppermute(kv_blk, 'ctx', shift_perm)
            run_state = fwd_update(run_state, q_five, kv_blk[0], kv_blk[1], block_mask(step_id), sm_scale)
            return kv_blk, run_state

        _, (m_run, l_run, o_acc) = lax.fori_loop(1, n_blocks + 1, fwd_body, ((k_loc, v_loc), state))
        log_sum = m_run + jnp.log(l_run)
        o_five = jnp.transpose((o_acc / l_run[..., None]).astype(jnp.bfloat16), (0, 3, 1, 2, 4))
        d_row = jnp.einsum('bqhgd,bqhgd->bhgq', do_five, o_five, preferred_element_type=jnp.float32)
        dq_acc, dk_acc, dv_acc = bwd_block(q_five, do_five, log_sum, d_row, k_loc, v_loc, block_mask(0), sm_scale)

        def bwd_body(step_id, carry):
            travel, dq_run = carry
            k_blk, v_blk, dk_run, dv_run = lax.ppermute(travel, 'ctx', shift_perm)
            dq_part, dk_part, dv_part = bwd_block(q_five, do_five, log_sum, d_row, k_blk, v_blk, block_mask(step_id), sm_scale)
            return (k_blk, v_blk, dk_run + dk_part, dv_run + dv_part), dq_run + dq_part

        (_, _, dk_acc, dv_acc), dq_acc = lax.fori_loop(1, n_blocks + 1, bwd_body, ((k_loc, v_loc, dk_acc, dv_acc), dq_acc))
        home_perm = [(j, (j - n_blocks) % n_ctx) for j in range(n_ctx)]
        dk_home, dv_home = lax.ppermute((dk_acc, dv_acc), 'ctx', home_perm)
        return (o_five.reshape(q_loc.shape), dq_acc.astype(jnp.bfloat16).reshape(q_loc.shape), dk_home.astype(jnp.bfloat16), dv_home.astype(jnp.bfloat16))

    return jax.shard_map(local_attn, mesh=mesh, in_specs=(seq_spec, seq_spec, seq_spec, seq_spec), out_specs=(seq_spec, seq_spec, seq_spec, seq_spec), check_vma=False)
```

profile of v0, /device:TPU:16, one launch (start us, length us, event | category | flops | bytes accessed | tf_op | source)
XLA Modules:
  0.0 392.7 jit_solution(9621824210996573294)
XLA Ops:
  4.8 113.4 %while.44 = (s32[]{:T(128)}, bf16[1,256,1,128]{3,1,2,0:T(8,128)(2,1)S(1)}, bf16[1,256,1,128]{3,1,2,0:T(8,128)(2,1)S(1)}, f32[1,1,4,256]{3,2,1,0:T(4,128)S(1)}, f...) while((s32[]{:T(128)}, ...), condition=%wide.region_5.6_spmd.clone, body=%wide.region_2.5_spmd.clone.sunk | while | flops 136711168 | bytes 5570767 | solution.py:64
  6.5 4.1 %collective-permute-done = bf16[1,256,1,128]{3,1,2,0:T(8,128)(2,1)S(1)} collective-permute-done((bf16[1,256,1,128]{3,1,2,0:T(8,128)(2,1)S(1)}, bf16[1,256,1,128]{3,1,2,0:T(8,128)(2,1)S(1)}, u32[]{:S(2)}, u32[]{:S(2)}) %collective-permute-start) | collective-permute-done | bytes 65568 | tf_op jit(solution)/shard_map/while/body/eval_jaxpr/ppermute | solution.py:60
  12.1 5.6 %collective-permute-done = bf16[1,256,1,128]{3,1,2,0:T(8,128)(2,1)S(1)} collective-permute-done((bf16[1,256,1,128]{3,1,2,0:T(8,128)(2,1)S(1)}, bf16[1,256,1,128]{3,1,2,0:T(8,128)(2,1)S(1)}, u32[]{:S(2)}, u32[]{:S(2)}) %collective-permute-start) | collective-permute-done | bytes 65568 | tf_op jit(solution)/shard_map/while/body/eval_jaxpr/ppermute | solution.py:60
  19.2 5.6 %collective-permute-done = bf16[1,256,1,128]{3,1,2,0:T(8,128)(2,1)S(1)} collective-permute-done((bf16[1,256,1,128]{3,1,2,0:T(8,128)(2,1)S(1)}, bf16[1,256,1,128]{3,1,2,0:T(8,128)(2,1)S(1)}, u32[]{:S(2)}, u32[]{:S(2)}) %collective-permute-start) | collective-permute-done | bytes 65568 | tf_op jit(solution)/shard_map/while/body/eval_jaxpr/ppermute | solution.py:60
  26.3 5.6 %collective-permute-done = bf16[1,256,1,128]{3,1,2,0:T(8,128)(2,1)S(1)} collective-permute-done((bf16[1,256,1,128]{3,1,2,0:T(8,128)(2,1)S(1)}, bf16[1,256,1,128]{3,1,2,0:T(8,128)(2,1)S(1)}, u32[]{:S(2)}, u32[]{:S(2)}) %collective-permute-start) | collective-permute-done | bytes 65568 | tf_op jit(solution)/shard_map/while/body/eval_jaxpr/ppermute | solution.py:60
  33.4 5.6 %collective-permute-done = bf16[1,256,1,128]{3,1,2,0:T(8,128)(2,1)S(1)} collective-permute-done((bf16[1,256,1,128]{3,1,2,0:T(8,128)(2,1)S(1)}, bf16[1,256,1,128]{3,1,2,0:T(8,128)(2,1)S(1)}, u32[]{:S(2)}, u32[]{:S(2)}) %collective-permute-start) | collective-permute-done | bytes 65568 | tf_op jit(solution)/shard_map/while/body/eval_jaxpr/ppermute | solution.py:60
  40.5 5.6 %collective-permute-done = bf16[1,256,1,128]{3,1,2,0:T(8,128)(2,1)S(1)} collective-permute-done((bf16[1,256,1,128]{3,1,2,0:T(8,128)(2,1)S(1)}, bf16[1,256,1,128]{3,1,2,0:T(8,128)(2,1)S(1)}, u32[]{:S(2)}, u32[]{:S(2)}) %collective-permute-start) | collective-permute-done | bytes 65568 | tf_op jit(solution)/shard_map/while/body/eval_jaxpr/ppermute | solution.py:60
  47.6 5.6 %collective-permute-done = bf16[1,256,1,128]{3,1,2,0:T(8,128)(2,1)S(1)} collective-permute-done((bf16[1,256,1,128]{3,1,2,0:T(8,128)(2,1)S(1)}, bf16[1,256,1,128]{3,1,2,0:T(8,128)(2,1)S(1)}, u32[]{:S(2)}, u32[]{:S(2)}) %collective-permute-start) | collective-permute-done | bytes 65568 | tf_op jit(solution)/shard_map/while/body/eval_jaxpr/ppermute | solution.py:60
  54.7 5.6 %collective-permute-done = bf16[1,256,1,128]{3,1,2,0:T(8,128)(2,1)S(1)} collective-permute-done((bf16[1,256,1,128]{3,1,2,0:T(8,128)(2,1)S(1)}, bf16[1,256,1,128]{3,1,2,0:T(8,128)(2,1)S(1)}, u32[]{:S(2)}, u32[]{:S(2)}) %collective-permute-start) | collective-permute-done | bytes 65568 | tf_op jit(solution)/shard_map/while/body/eval_jaxpr/ppermute | solution.py:60
  61.8 5.6 %collective-permute-done = bf16[1,256,1,128]{3,1,2,0:T(8,128)(2,1)S(1)} collective-permute-done((bf16[1,256,1,128]{3,1,2,0:T(8,128)(2,1)S(1)}, bf16[1,256,1,128]{3,1,2,0:T(8,128)(2,1)S(1)}, u32[]{:S(2)}, u32[]{:S(2)}) %collective-permute-start) | collective-permute-done | bytes 65568 | tf_op jit(solution)/shard_map/while/body/eval_jaxpr/ppermute | solution.py:60
  68.9 5.6 %collective-permute-done = bf16[1,256,1,128]{3,1,2,0:T(8,128)(2,1)S(1)} collective-permute-done((bf16[1,256,1,128]{3,1,2,0:T(8,128)(2,1)S(1)}, bf16[1,256,1,128]{3,1,2,0:T(8,128)(2,1)S(1)}, u32[]{:S(2)}, u32[]{:S(2)}) %collective-permute-start) | collective-permute-done | bytes 65568 | tf_op jit(solution)/shard_map/while/body/eval_jaxpr/ppermute | solution.py:60
  76.0 5.6 %collective-permute-done = bf16[1,256,1,128]{3,1,2,0:T(8,128)(2,1)S(1)} collective-permute-done((bf16[1,256,1,128]{3,1,2,0:T(8,128)(2,1)S(1)}, bf16[1,256,1,128]{3,1,2,0:T(8,128)(2,1)S(1)}, u32[]{:S(2)}, u32[]{:S(2)}) %collective-permute-start) | collective-permute-done | bytes 65568 | tf_op jit(solution)/shard_map/while/body/eval_jaxpr/ppermute | solution.py:60
  83.1 5.6 %collective-permute-done = bf16[1,256,1,128]{3,1,2,0:T(8,128)(2,1)S(1)} collective-permute-done((bf16[1,256,1,128]{3,1,2,0:T(8,128)(2,1)S(1)}, bf16[1,256,1,128]{3,1,2,0:T(8,128)(2,1)S(1)}, u32[]{:S(2)}, u32[]{:S(2)}) %collective-permute-start) | collective-permute-done | bytes 65568 | tf_op jit(solution)/shard_map/while/body/eval_jaxpr/ppermute | solution.py:60
  90.2 5.6 %collective-permute-done = bf16[1,256,1,128]{3,1,2,0:T(8,128)(2,1)S(1)} collective-permute-done((bf16[1,256,1,128]{3,1,2,0:T(8,128)(2,1)S(1)}, bf16[1,256,1,128]{3,1,2,0:T(8,128)(2,1)S(1)}, u32[]{:S(2)}, u32[]{:S(2)}) %collective-permute-start) | collective-permute-done | bytes 65568 | tf_op jit(solution)/shard_map/while/body/eval_jaxpr/ppermute | solution.py:60
  97.3 5.6 %collective-permute-done = bf16[1,256,1,128]{3,1,2,0:T(8,128)(2,1)S(1)} collective-permute-done((bf16[1,256,1,128]{3,1,2,0:T(8,128)(2,1)S(1)}, bf16[1,256,1,128]{3,1,2,0:T(8,128)(2,1)S(1)}, u32[]{:S(2)}, u32[]{:S(2)}) %collective-permute-start) | collective-permute-done | bytes 65568 | tf_op jit(solution)/shard_map/while/body/eval_jaxpr/ppermute | solution.py:60
  104.4 5.6 %collective-permute-done = bf16[1,256,1,128]{3,1,2,0:T(8,128)(2,1)S(1)} collective-permute-done((bf16[1,256,1,128]{3,1,2,0:T(8,128)(2,1)S(1)}, bf16[1,256,1,128]{3,1,2,0:T(8,128)(2,1)S(1)}, u32[]{:S(2)}, u32[]{:S(2)}) %collective-permute-start) | collective-permute-done | bytes 65568 | tf_op jit(solution)/shard_map/while/body/eval_jaxpr/ppermute | solution.py:60
  111.5 5.6 %collective-permute-done = bf16[1,256,1,128]{3,1,2,0:T(8,128)(2,1)S(1)} collective-permute-done((bf16[1,256,1,128]{3,1,2,0:T(8,128)(2,1)S(1)}, bf16[1,256,1,128]{3,1,2,0:T(8,128)(2,1)S(1)}, u32[]{:S(2)}, u32[]{:S(2)}) %collective-permute-start) | collective-permute-done | bytes 65568 | tf_op jit(solution)/shard_map/while/body/eval_jaxpr/ppermute | solution.py:60
  122.1 197.0 %while.45 = (s32[]{:T(128)}, bf16[1,256,1,128]{3,1,2,0:T(8,128)(2,1)S(1)}, bf16[1,256,1,128]{3,1,2,0:T(8,128)(2,1)S(1)}, f32[1,256,1,128]{3,1,2,0:T(8,128)S(1)},...) while((s32[]{:T(128)}, ...), condition=%wide.region_7.8_spmd.clone, body=%wide.region_6.7_spmd.clone.sunk | while | flops 338132992 | bytes 9511223 | solution.py:76
  122.5 5.4 %collective-permute-done.2 = bf16[1,256,1,128]{3,1,2,0:T(8,128)(2,1)S(1)} collective-permute-done((bf16[1,256,1,128]{3,1,2,0:T(8,128)(2,1)S(1)}, bf16[1,256,1,128]{3,1,2,0:T(8,128)(2,1)S(1)}, u32[]{:S(2)}, u32[]{:S(2)}) %collective-permute-start.2) | collective-permute-done | bytes 65568 | tf_op jit(solution)/shard_map/while/body/eval_jaxpr/ppermute | solution.py:72
  132.0 2.5 collective-permute-start.4
  134.4 4.5 %collective-permute-start.5 = (f32[1,256,1,128]{3,1,2,0:T(8,128)S(1)}, f32[1,256,1,128]{3,1,2,0:T(8,128)S(1)}, u32[]{:S(2)}, u32[]{:S(2)}) collective-permute-start(f32[1,256,1,128]{3,1,2,0:T(8,128)S(1)} %get-tuple-element.631), channel_id=1, source_target_pairs={{0,1},{1,2},{2,3},{3,4},{4,5},{5,6},{6,7},{7,8},{8,9},{9,10},{10,1... | collective-permute-start | bytes 393224 | tf_op jit(solution)/shard_map/while/body/eval_jaxpr/ppermute | solution.py:72
  141.5 2.6 collective-permute-start.2
  144.0 4.5 %collective-permute-start.3 = (bf16[1,256,1,128]{3,1,2,0:T(8,128)(2,1)S(1)}, bf16[1,256,1,128]{3,1,2,0:T(8,128)(2,1)S(1)}, u32[]{:S(2)}, u32[]{:S(2)}) collective-permute-start(bf16[1,256,1,128]{3,1,2,0:T(8,128)(2,1)S(1)} %get-tuple-element.629), channel_id=1, source_target_pairs={{0,1},{1,2},{2,3},{3,4},{4,5},{5,6},{6,7},{7,8},{8,9},{9,10},{10,1... | collective-permute-start | bytes 196616 | tf_op jit(solution)/shard_map/while/body/eval_jaxpr/ppermute | solution.py:72
  148.6 2.8 collective-permute-start.4
  151.3 4.9 %collective-permute-start.5 = (f32[1,256,1,128]{3,1,2,0:T(8,128)S(1)}, f32[1,256,1,128]{3,1,2,0:T(8,128)S(1)}, u32[]{:S(2)}, u32[]{:S(2)}) collective-permute-start(f32[1,256,1,128]{3,1,2,0:T(8,128)S(1)} %get-tuple-element.631), channel_id=1, source_target_pairs={{0,1},{1,2},{2,3},{3,4},{4,5},{5,6},{6,7},{7,8},{8,9},{9,10},{10,1... | collective-permute-start | bytes 393224 | tf_op jit(solution)/shard_map/while/body/eval_jaxpr/ppermute | solution.py:72
  158.1 2.8 collective-permute-start.2
  160.9 4.9 %collective-permute-start.3 = (bf16[1,256,1,128]{3,1,2,0:T(8,128)(2,1)S(1)}, bf16[1,256,1,128]{3,1,2,0:T(8,128)(2,1)S(1)}, u32[]{:S(2)}, u32[]{:S(2)}) collective-permute-start(bf16[1,256,1,128]{3,1,2,0:T(8,128)(2,1)S(1)} %get-tuple-element.629), channel_id=1, source_target_pairs={{0,1},{1,2},{2,3},{3,4},{4,5},{5,6},{6,7},{7,8},{8,9},{9,10},{10,1... | collective-permute-start | bytes 196616 | tf_op jit(solution)/shard_map/while/body/eval_jaxpr/ppermute | solution.py:72
  165.9 2.6 collective-permute-start.4
  168.5 5.1 %collective-permute-start.5 = (f32[1,256,1,128]{3,1,2,0:T(8,128)S(1)}, f32[1,256,1,128]{3,1,2,0:T(8,128)S(1)}, u32[]{:S(2)}, u32[]{:S(2)}) collective-permute-start(f32[1,256,1,128]{3,1,2,0:T(8,128)S(1)} %get-tuple-element.631), channel_id=1, source_target_pairs={{0,1},{1,2},{2,3},{3,4},{4,5},{5,6},{6,7},{7,8},{8,9},{9,10},{10,1... | collective-permute-start | bytes 393224 | tf_op jit(solution)/shard_map/while/body/eval_jaxpr/ppermute | solution.py:72
  175.4 3.1 collective-permute-start.2
  182.4 4.1 %collective-permute-start.5 = (f32[1,256,1,128]{3,1,2,0:T(8,128)S(1)}, f32[1,256,1,128]{3,1,2,0:T(8,128)S(1)}, u32[]{:S(2)}, u32[]{:S(2)}) collective-permute-start(f32[1,256,1,128]{3,1,2,0:T(8,128)S(1)} %get-tuple-element.631), channel_id=1, source_target_pairs={{0,1},{1,2},{2,3},{3,4},{4,5},{5,6},{6,7},{7,8},{8,9},{9,10},{10,1... | collective-permute-start | bytes 393224 | tf_op jit(solution)/shard_map/while/body/eval_jaxpr/ppermute | solution.py:72
  190.6 2.4 collective-permute-start.3
  194.4 3.8 collective-permute-start.5
  206.2 3.8 collective-permute-start.5
  214.2 2.4 collective-permute-start.3
  218.0 3.8 collective-permute-start.5
  226.0 2.4 collective-permute-start.3
  229.8 3.8 collective-permute-start.5
  237.8 2.4 collective-permute-start.3
  241.6 3.8 collective-permute-start.5
  253.4 3.8 collective-permute-start.5
  265.2 3.8 collective-permute-start.5
  277.0 3.8 collective-permute-start.5
  288.8 3.8 collective-permute-start.5
  300.6 3.8 collective-permute-start.5
  312.3 3.8 collective-permute-start.5
  319.2 65.5 %collective-permute-start.6 = (bf16[1,256,1,128]{3,1,2,0:T(8,128)(2,1)S(1)}, bf16[1,256,1,128]{3,1,2,0:T(8,128)(2,1)S(1)}, u32[]{:S(2)}, u32[]{:S(2)}) collective-permute-start(bf16[1,256,1,128]{3,1,2,0:T(8,128)(2,1)S(1)} %convert.15), channel_id=1, source_target_pairs={{0,112},{1,113},{2,114},{3,115},{4,116},{5,117},{6,118},{7,119},{8... | collective-permute-start | bytes 196616 | tf_op jit(solution)/shard_map/ppermute | solution.py:78
  386.6 4.8 %collective-permute-done.7 = bf16[1,256,1,128]{3,1,2,0:T(8,128)(2,1)S(1)} collective-permute-done((bf16[1,256,1,128]{3,1,2,0:T(8,128)(2,1)S(1)}, bf16[1,256,1,128]{3,1,2,0:T(8,128)(2,1)S(1)}, u32[]{:S(2)}, u32[]{:S(2)}) %collective-permute-start.7) | collective-permute-done | bytes 65568 | tf_op jit(solution)/shard_map/ppermute | solution.py:78
  (461 shorter events, 128.8 us)
Async XLA Ops:
  122.3 7.8 %collective-permute-start.4 = (f32[1,256,1,128]{3,1,2,0:T(8,128)S(1)}, f32[1,256,1,128]{3,1,2,0:T(8,128)S(1)}, u32[]{:S(2)}, u32[]{:S(2)}) collective-permute-start(f32[1,256,1,128]{3,1,2,0:T(8,128)S(1)} %get-tuple-element.630), channel_id=1, source_target_pairs={{0,1},{1,2},{2,3},{3,4},{4,5},{5,6},{6,7},{7,8},{8,9},{9,10},{10,1... | collective-permute-start | bytes 393224 | tf_op jit(solution)/shard_map/while/body/eval_jaxpr/ppermute | solution.py:72
  122.4 9.1 %collective-permute-start.5 = (f32[1,256,1,128]{3,1,2,0:T(8,128)S(1)}, f32[1,256,1,128]{3,1,2,0:T(8,128)S(1)}, u32[]{:S(2)}, u32[]{:S(2)}) collective-permute-start(f32[1,256,1,128]{3,1,2,0:T(8,128)S(1)} %get-tuple-element.631), channel_id=1, source_target_pairs={{0,1},{1,2},{2,3},{3,4},{4,5},{5,6},{6,7},{7,8},{8,9},{9,10},{10,1... | collective-permute-start | bytes 393224 | tf_op jit(solution)/shard_map/while/body/eval_jaxpr/ppermute | solution.py:72
  131.8 7.2 %collective-permute-start.2 = (bf16[1,256,1,128]{3,1,2,0:T(8,128)(2,1)S(1)}, bf16[1,256,1,128]{3,1,2,0:T(8,128)(2,1)S(1)}, u32[]{:S(2)}, u32[]{:S(2)}) collective-permute-start(bf16[1,256,1,128]{3,1,2,0:T(8,128)(2,1)S(1)} %get-tuple-element.628), channel_id=1, source_target_pairs={{0,1},{1,2},{2,3},{3,4},{4,5},{5,6},{6,7},{7,8},{8,9},{9,10},{10,1... | collective-permute-start | bytes 196616 | tf_op jit(solution)/shard_map/while/body/eval_jaxpr/ppermute | solution.py:72
  131.9 7.6 %collective-permute-start.3 = (bf16[1,256,1,128]{3,1,2,0:T(8,128)(2,1)S(1)}, bf16[1,256,1,128]{3,1,2,0:T(8,128)(2,1)S(1)}, u32[]{:S(2)}, u32[]{:S(2)}) collective-permute-start(bf16[1,256,1,128]{3,1,2,0:T(8,128)(2,1)S(1)} %get-tuple-element.629), channel_id=1, source_target_pairs={{0,1},{1,2},{2,3},{3,4},{4,5},{5,6},{6,7},{7,8},{8,9},{9,10},{10,1... | collective-permute-start | bytes 196616 | tf_op jit(solution)/shard_map/while/body/eval_jaxpr/ppermute | solution.py:72
  132.0 8.2 %collective-permute-start.4 = (f32[1,256,1,128]{3,1,2,0:T(8,128)S(1)}, f32[1,256,1,128]{3,1,2,0:T(8,128)S(1)}, u32[]{:S(2)}, u32[]{:S(2)}) collective-permute-start(f32[1,256,1,128]{3,1,2,0:T(8,128)S(1)} %get-tuple-element.630), channel_id=1, source_target_pairs={{0,1},{1,2},{2,3},{3,4},{4,5},{5,6},{6,7},{7,8},{8,9},{9,10},{10,1... | collective-permute-start | bytes 393224 | tf_op jit(solution)/shard_map/while/body/eval_jaxpr/ppermute | solution.py:72
  134.4 6.7 %collective-permute-start.5 = (f32[1,256,1,128]{3,1,2,0:T(8,128)S(1)}, f32[1,256,1,128]{3,1,2,0:T(8,128)S(1)}, u32[]{:S(2)}, u32[]{:S(2)}) collective-permute-start(f32[1,256,1,128]{3,1,2,0:T(8,128)S(1)} %get-tuple-element.631), channel_id=1, source_target_pairs={{0,1},{1,2},{2,3},{3,4},{4,5},{5,6},{6,7},{7,8},{8,9},{9,10},{10,1... | collective-permute-start | bytes 393224 | tf_op jit(solution)/shard_map/while/body/eval_jaxpr/ppermute | solution.py:72
  141.5 14.9 %collective-permute-start.2 = (bf16[1,256,1,128]{3,1,2,0:T(8,128)(2,1)S(1)}, bf16[1,256,1,128]{3,1,2,0:T(8,128)(2,1)S(1)}, u32[]{:S(2)}, u32[]{:S(2)}) collective-permute-start(bf16[1,256,1,128]{3,1,2,0:T(8,128)(2,1)S(1)} %get-tuple-element.628), channel_id=1, source_target_pairs={{0,1},{1,2},{2,3},{3,4},{4,5},{5,6},{6,7},{7,8},{8,9},{9,10},{10,1... | collective-permute-start | bytes 196616 | tf_op jit(solution)/shard_map/while/body/eval_jaxpr/ppermute | solution.py:72
  144.0 12.7 %collective-permute-start.3 = (bf16[1,256,1,128]{3,1,2,0:T(8,128)(2,1)S(1)}, bf16[1,256,1,128]{3,1,2,0:T(8,128)(2,1)S(1)}, u32[]{:S(2)}, u32[]{:S(2)}) collective-permute-start(bf16[1,256,1,128]{3,1,2,0:T(8,128)(2,1)S(1)} %get-tuple-element.629), channel_id=1, source_target_pairs={{0,1},{1,2},{2,3},{3,4},{4,5},{5,6},{6,7},{7,8},{8,9},{9,10},{10,1... | collective-permute-start | bytes 196616 | tf_op jit(solution)/shard_map/while/body/eval_jaxpr/ppermute | solution.py:72
  148.6 8.9 %collective-permute-start.4 = (f32[1,256,1,128]{3,1,2,0:T(8,128)S(1)}, f32[1,256,1,128]{3,1,2,0:T(8,128)S(1)}, u32[]{:S(2)}, u32[]{:S(2)}) collective-permute-start(f32[1,256,1,128]{3,1,2,0:T(8,128)S(1)} %get-tuple-element.630), channel_id=1, source_target_pairs={{0,1},{1,2},{2,3},{3,4},{4,5},{5,6},{6,7},{7,8},{8,9},{9,10},{10,1... | collective-permute-start | bytes 393224 | tf_op jit(solution)/shard_map/while/body/eval_jaxpr/ppermute | solution.py:72
  158.1 15.5 %collective-permute-start.2 = (bf16[1,256,1,128]{3,1,2,0:T(8,128)(2,1)S(1)}, bf16[1,256,1,128]{3,1,2,0:T(8,128)(2,1)S(1)}, u32[]{:S(2)}, u32[]{:S(2)}) collective-permute-start(bf16[1,256,1,128]{3,1,2,0:T(8,128)(2,1)S(1)} %get-tuple-element.628), channel_id=1, source_target_pairs={{0,1},{1,2},{2,3},{3,4},{4,5},{5,6},{6,7},{7,8},{8,9},{9,10},{10,1... | collective-permute-start | bytes 196616 | tf_op jit(solution)/shard_map/while/body/eval_jaxpr/ppermute | solution.py:72
  160.9 13.1 %collective-permute-start.3 = (bf16[1,256,1,128]{3,1,2,0:T(8,128)(2,1)S(1)}, bf16[1,256,1,128]{3,1,2,0:T(8,128)(2,1)S(1)}, u32[]{:S(2)}, u32[]{:S(2)}) collective-permute-start(bf16[1,256,1,128]{3,1,2,0:T(8,128)(2,1)S(1)} %get-tuple-element.629), channel_id=1, source_target_pairs={{0,1},{1,2},{2,3},{3,4},{4,5},{5,6},{6,7},{7,8},{8,9},{9,10},{10,1... | collective-permute-start | bytes 196616 | tf_op jit(solution)/shard_map/while/body/eval_jaxpr/ppermute | solution.py:72
  165.9 8.9 %collective-permute-start.4 = (f32[1,256,1,128]{3,1,2,0:T(8,128)S(1)}, f32[1,256,1,128]{3,1,2,0:T(8,128)S(1)}, u32[]{:S(2)}, u32[]{:S(2)}) collective-permute-start(f32[1,256,1,128]{3,1,2,0:T(8,128)S(1)} %get-tuple-element.630), channel_id=1, source_target_pairs={{0,1},{1,2},{2,3},{3,4},{4,5},{5,6},{6,7},{7,8},{8,9},{9,10},{10,1... | collective-permute-start | bytes 393224 | tf_op jit(solution)/shard_map/while/body/eval_jaxpr/ppermute | solution.py:72
  168.5 6.6 %collective-permute-start.5 = (f32[1,256,1,128]{3,1,2,0:T(8,128)S(1)}, f32[1,256,1,128]{3,1,2,0:T(8,128)S(1)}, u32[]{:S(2)}, u32[]{:S(2)}) collective-permute-start(f32[1,256,1,128]{3,1,2,0:T(8,128)S(1)} %get-tuple-element.631), channel_id=1, source_target_pairs={{0,1},{1,2},{2,3},{3,4},{4,5},{5,6},{6,7},{7,8},{8,9},{9,10},{10,1... | collective-permute-start | bytes 393224 | tf_op jit(solution)/shard_map/while/body/eval_jaxpr/ppermute | solution.py:72
  175.4 11.2 %collective-permute-start.2 = (bf16[1,256,1,128]{3,1,2,0:T(8,128)(2,1)S(1)}, bf16[1,256,1,128]{3,1,2,0:T(8,128)(2,1)S(1)}, u32[]{:S(2)}, u32[]{:S(2)}) collective-permute-start(bf16[1,256,1,128]{3,1,2,0:T(8,128)(2,1)S(1)} %get-tuple-element.628), channel_id=1, source_target_pairs={{0,1},{1,2},{2,3},{3,4},{4,5},{5,6},{6,7},{7,8},{8,9},{9,10},{10,1... | collective-permute-start | bytes 196616 | tf_op jit(solution)/shard_map/while/body/eval_jaxpr/ppermute | solution.py:72
  178.5 8.5 %collective-permute-start.3 = (bf16[1,256,1,128]{3,1,2,0:T(8,128)(2,1)S(1)}, bf16[1,256,1,128]{3,1,2,0:T(8,128)(2,1)S(1)}, u32[]{:S(2)}, u32[]{:S(2)}) collective-permute-start(bf16[1,256,1,128]{3,1,2,0:T(8,128)(2,1)S(1)} %get-tuple-element.629), channel_id=1, source_target_pairs={{0,1},{1,2},{2,3},{3,4},{4,5},{5,6},{6,7},{7,8},{8,9},{9,10},{10,1... | collective-permute-start | bytes 196616 | tf_op jit(solution)/shard_map/while/body/eval_jaxpr/ppermute | solution.py:72
  181.0 6.7 %collective-permute-start.4 = (f32[1,256,1,128]{3,1,2,0:T(8,128)S(1)}, f32[1,256,1,128]{3,1,2,0:T(8,128)S(1)}, u32[]{:S(2)}, u32[]{:S(2)}) collective-permute-start(f32[1,256,1,128]{3,1,2,0:T(8,128)S(1)} %get-tuple-element.630), channel_id=1, source_target_pairs={{0,1},{1,2},{2,3},{3,4},{4,5},{5,6},{6,7},{7,8},{8,9},{9,10},{10,1... | collective-permute-start | bytes 393224 | tf_op jit(solution)/shard_map/while/body/eval_jaxpr/ppermute | solution.py:72
  189.2 9.2 %collective-permute-start.2 = (bf16[1,256,1,128]{3,1,2,0:T(8,128)(2,1)S(1)}, bf16[1,256,1,128]{3,1,2,0:T(8,128)(2,1)S(1)}, u32[]{:S(2)}, u32[]{:S(2)}) collective-permute-start(bf16[1,256,1,128]{3,1,2,0:T(8,128)(2,1)S(1)} %get-tuple-element.628), channel_id=1, source_target_pairs={{0,1},{1,2},{2,3},{3,4},{4,5},{5,6},{6,7},{7,8},{8,9},{9,10},{10,1... | collective-permute-start | bytes 196616 | tf_op jit(solution)/shard_map/while/body/eval_jaxpr/ppermute | solution.py:72
  190.6 8.2 %collective-permute-start.3 = (bf16[1,256,1,128]{3,1,2,0:T(8,128)(2,1)S(1)}, bf16[1,256,1,128]{3,1,2,0:T(8,128)(2,1)S(1)}, u32[]{:S(2)}, u32[]{:S(2)}) collective-permute-start(bf16[1,256,1,128]{3,1,2,0:T(8,128)(2,1)S(1)} %get-tuple-element.629), channel_id=1, source_target_pairs={{0,1},{1,2},{2,3},{3,4},{4,5},{5,6},{6,7},{7,8},{8,9},{9,10},{10,1... | collective-permute-start | bytes 196616 | tf_op jit(solution)/shard_map/while/body/eval_jaxpr/ppermute | solution.py:72
  194.4 6.5 %collective-permute-start.5 = (f32[1,256,1,128]{3,1,2,0:T(8,128)S(1)}, f32[1,256,1,128]{3,1,2,0:T(8,128)S(1)}, u32[]{:S(2)}, u32[]{:S(2)}) collective-permute-start(f32[1,256,1,128]{3,1,2,0:T(8,128)S(1)} %get-tuple-element.631), channel_id=1, source_target_pairs={{0,1},{1,2},{2,3},{3,4},{4,5},{5,6},{6,7},{7,8},{8,9},{9,10},{10,1... | collective-permute-start | bytes 393224 | tf_op jit(solution)/shard_map/while/body/eval_jaxpr/ppermute | solution.py:72
  201.3 8.9 %collective-permute-start.2 = (bf16[1,256,1,128]{3,1,2,0:T(8,128)(2,1)S(1)}, bf16[1,256,1,128]{3,1,2,0:T(8,128)(2,1)S(1)}, u32[]{:S(2)}, u32[]{:S(2)}) collective-permute-start(bf16[1,256,1,128]{3,1,2,0:T(8,128)(2,1)S(1)} %get-tuple-element.628), channel_id=1, source_target_pairs={{0,1},{1,2},{2,3},{3,4},{4,5},{5,6},{6,7},{7,8},{8,9},{9,10},{10,1... | collective-permute-start | bytes 196616 | tf_op jit(solution)/shard_map/while/body/eval_jaxpr/ppermute | solution.py:72
  202.4 8.2 %collective-permute-start.3 = (bf16[1,256,1,128]{3,1,2,0:T(8,128)(2,1)S(1)}, bf16[1,256,1,128]{3,1,2,0:T(8,128)(2,1)S(1)}, u32[]{:S(2)}, u32[]{:S(2)}) collective-permute-start(bf16[1,256,1,128]{3,1,2,0:T(8,128)(2,1)S(1)} %get-tuple-element.629), channel_id=1, source_target_pairs={{0,1},{1,2},{2,3},{3,4},{4,5},{5,6},{6,7},{7,8},{8,9},{9,10},{10,1... | collective-permute-start | bytes 196616 | tf_op jit(solution)/shard_map/while/body/eval_jaxpr/ppermute | solution.py:72
  213.0 8.9 %collective-permute-start.2 = (bf16[1,256,1,128]{3,1,2,0:T(8,128)(2,1)S(1)}, bf16[1,256,1,128]{3,1,2,0:T(8,128)(2,1)S(1)}, u32[]{:S(2)}, u32[]{:S(2)}) collective-permute-start(bf16[1,256,1,128]{3,1,2,0:T(8,128)(2,1)S(1)} %get-tuple-element.628), channel_id=1, source_target_pairs={{0,1},{1,2},{2,3},{3,4},{4,5},{5,6},{6,7},{7,8},{8,9},{9,10},{10,1... | collective-permute-start | bytes 196616 | tf_op jit(solution)/shard_map/while/body/eval_jaxpr/ppermute | solution.py:72
  214.2 8.2 %collective-permute-start.3 = (bf16[1,256,1,128]{3,1,2,0:T(8,128)(2,1)S(1)}, bf16[1,256,1,128]{3,1,2,0:T(8,128)(2,1)S(1)}, u32[]{:S(2)}, u32[]{:S(2)}) collective-permute-start(bf16[1,256,1,128]{3,1,2,0:T(8,128)(2,1)S(1)} %get-tuple-element.629), channel_id=1, source_target_pairs={{0,1},{1,2},{2,3},{3,4},{4,5},{5,6},{6,7},{7,8},{8,9},{9,10},{10,1... | collective-permute-start | bytes 196616 | tf_op jit(solution)/shard_map/while/body/eval_jaxpr/ppermute | solution.py:72
  224.8 8.9 %collective-permute-start.2 = (bf16[1,256,1,128]{3,1,2,0:T(8,128)(2,1)S(1)}, bf16[1,256,1,128]{3,1,2,0:T(8,128)(2,1)S(1)}, u32[]{:S(2)}, u32[]{:S(2)}) collective-permute-start(bf16[1,256,1,128]{3,1,2,0:T(8,128)(2,1)S(1)} %get-tuple-element.628), channel_id=1, source_target_pairs={{0,1},{1,2},{2,3},{3,4},{4,5},{5,6},{6,7},{7,8},{8,9},{9,10},{10,1... | collective-permute-start | bytes 196616 | tf_op jit(solution)/shard_map/while/body/eval_jaxpr/ppermute | solution.py:72
  226.0 8.2 %collective-permute-start.3 = (bf16[1,256,1,128]{3,1,2,0:T(8,128)(2,1)S(1)}, bf16[1,256,1,128]{3,1,2,0:T(8,128)(2,1)S(1)}, u32[]{:S(2)}, u32[]{:S(2)}) collective-permute-start(bf16[1,256,1,128]{3,1,2,0:T(8,128)(2,1)S(1)} %get-tuple-element.629), channel_id=1, source_target_pairs={{0,1},{1,2},{2,3},{3,4},{4,5},{5,6},{6,7},{7,8},{8,9},{9,10},{10,1... | collective-permute-start | bytes 196616 | tf_op jit(solution)/shard_map/while/body/eval_jaxpr/ppermute | solution.py:72
  229.8 6.5 %collective-permute-start.5 = (f32[1,256,1,128]{3,1,2,0:T(8,128)S(1)}, f32[1,256,1,128]{3,1,2,0:T(8,128)S(1)}, u32[]{:S(2)}, u32[]{:S(2)}) collective-permute-start(f32[1,256,1,128]{3,1,2,0:T(8,128)S(1)} %get-tuple-element.631), channel_id=1, source_target_pairs={{0,1},{1,2},{2,3},{3,4},{4,5},{5,6},{6,7},{7,8},{8,9},{9,10},{10,1... | collective-permute-start | bytes 393224 | tf_op jit(solution)/shard_map/while/body/eval_jaxpr/ppermute | solution.py:72
  236.6 8.9 %collective-permute-start.2 = (bf16[1,256,1,128]{3,1,2,0:T(8,128)(2,1)S(1)}, bf16[1,256,1,128]{3,1,2,0:T(8,128)(2,1)S(1)}, u32[]{:S(2)}, u32[]{:S(2)}) collective-permute-start(bf16[1,256,1,128]{3,1,2,0:T(8,128)(2,1)S(1)} %get-tuple-element.628), channel_id=1, source_target_pairs={{0,1},{1,2},{2,3},{3,4},{4,5},{5,6},{6,7},{7,8},{8,9},{9,10},{10,1... | collective-permute-start | bytes 196616 | tf_op jit(solution)/shard_map/while/body/eval_jaxpr/ppermute | solution.py:72
  237.8 8.2 %collective-permute-start.3 = (bf16[1,256,1,128]{3,1,2,0:T(8,128)(2,1)S(1)}, bf16[1,256,1,128]{3,1,2,0:T(8,128)(2,1)S(1)}, u32[]{:S(2)}, u32[]{:S(2)}) collective-permute-start(bf16[1,256,1,128]{3,1,2,0:T(8,128)(2,1)S(1)} %get-tuple-element.629), channel_id=1, source_target_pairs={{0,1},{1,2},{2,3},{3,4},{4,5},{5,6},{6,7},{7,8},{8,9},{9,10},{10,1... | collective-permute-start | bytes 196616 | tf_op jit(solution)/shard_map/while/body/eval_jaxpr/ppermute | solution.py:72
  241.6 6.5 %collective-permute-start.5 = (f32[1,256,1,128]{3,1,2,0:T(8,128)S(1)}, f32[1,256,1,128]{3,1,2,0:T(8,128)S(1)}, u32[]{:S(2)}, u32[]{:S(2)}) collective-permute-start(f32[1,256,1,128]{3,1,2,0:T(8,128)S(1)} %get-tuple-element.631), channel_id=1, source_target_pairs={{0,1},{1,2},{2,3},{3,4},{4,5},{5,6},{6,7},{7,8},{8,9},{9,10},{10,1... | collective-permute-start | bytes 393224 | tf_op jit(solution)/shard_map/while/body/eval_jaxpr/ppermute | solution.py:72
  248.4 8.9 %collective-permute-start.2 = (bf16[1,256,1,128]{3,1,2,0:T(8,128)(2,1)S(1)}, bf16[1,256,1,128]{3,1,2,0:T(8,128)(2,1)S(1)}, u32[]{:S(2)}, u32[]{:S(2)}) collective-permute-start(bf16[1,256,1,128]{3,1,2,0:T(8,128)(2,1)S(1)} %get-tuple-element.628), channel_id=1, source_target_pairs={{0,1},{1,2},{2,3},{3,4},{4,5},{5,6},{6,7},{7,8},{8,9},{9,10},{10,1... | collective-permute-start | bytes 196616 | tf_op jit(solution)/shard_map/while/body/eval_jaxpr/ppermute | solution.py:72
  249.5 8.2 %collective-permute-start.3 = (bf16[1,256,1,128]{3,1,2,0:T(8,128)(2,1)S(1)}, bf16[1,256,1,128]{3,1,2,0:T(8,128)(2,1)S(1)}, u32[]{:S(2)}, u32[]{:S(2)}) collective-permute-start(bf16[1,256,1,128]{3,1,2,0:T(8,128)(2,1)S(1)} %get-tuple-element.629), channel_id=1, source_target_pairs={{0,1},{1,2},{2,3},{3,4},{4,5},{5,6},{6,7},{7,8},{8,9},{9,10},{10,1... | collective-permute-start | bytes 196616 | tf_op jit(solution)/shard_map/while/body/eval_jaxpr/ppermute | solution.py:72
  253.4 6.5 %collective-permute-start.5 = (f32[1,256,1,128]{3,1,2,0:T(8,128)S(1)}, f32[1,256,1,128]{3,1,2,0:T(8,128)S(1)}, u32[]{:S(2)}, u32[]{:S(2)}) collective-permute-start(f32[1,256,1,128]{3,1,2,0:T(8,128)S(1)} %get-tuple-element.631), channel_id=1, source_target_pairs={{0,1},{1,2},{2,3},{3,4},{4,5},{5,6},{6,7},{7,8},{8,9},{9,10},{10,1... | collective-permute-start | bytes 393224 | tf_op jit(solution)/shard_map/while/body/eval_jaxpr/ppermute | solution.py:72
  260.2 8.9 %collective-permute-start.2 = (bf16[1,256,1,128]{3,1,2,0:T(8,128)(2,1)S(1)}, bf16[1,256,1,128]{3,1,2,0:T(8,128)(2,1)S(1)}, u32[]{:S(2)}, u32[]{:S(2)}) collective-permute-start(bf16[1,256,1,128]{3,1,2,0:T(8,128)(2,1)S(1)} %get-tuple-element.628), channel_id=1, source_target_pairs={{0,1},{1,2},{2,3},{3,4},{4,5},{5,6},{6,7},{7,8},{8,9},{9,10},{10,1... | collective-permute-start | bytes 196616 | tf_op jit(solution)/shard_map/while/body/eval_jaxpr/ppermute | solution.py:72
  261.3 8.2 %collective-permute-start.3 = (bf16[1,256,1,128]{3,1,2,0:T(8,128)(2,1)S(1)}, bf16[1,256,1,128]{3,1,2,0:T(8,128)(2,1)S(1)}, u32[]{:S(2)}, u32[]{:S(2)}) collective-permute-start(bf16[1,256,1,128]{3,1,2,0:T(8,128)(2,1)S(1)} %get-tuple-element.629), channel_id=1, source_target_pairs={{0,1},{1,2},{2,3},{3,4},{4,5},{5,6},{6,7},{7,8},{8,9},{9,10},{10,1... | collective-permute-start | bytes 196616 | tf_op jit(solution)/shard_map/while/body/eval_jaxpr/ppermute | solution.py:72
  265.2 6.5 %collective-permute-start.5 = (f32[1,256,1,128]{3,1,2,0:T(8,128)S(1)}, f32[1,256,1,128]{3,1,2,0:T(8,128)S(1)}, u32[]{:S(2)}, u32[]{:S(2)}) collective-permute-start(f32[1,256,1,128]{3,1,2,0:T(8,128)S(1)} %get-tuple-element.631), channel_id=1, source_target_pairs={{0,1},{1,2},{2,3},{3,4},{4,5},{5,6},{6,7},{7,8},{8,9},{9,10},{10,1... | collective-permute-start | bytes 393224 | tf_op jit(solution)/shard_map/while/body/eval_jaxpr/ppermute | solution.py:72
  272.0 8.9 %collective-permute-start.2 = (bf16[1,256,1,128]{3,1,2,0:T(8,128)(2,1)S(1)}, bf16[1,256,1,128]{3,1,2,0:T(8,128)(2,1)S(1)}, u32[]{:S(2)}, u32[]{:S(2)}) collective-permute-start(bf16[1,256,1,128]{3,1,2,0:T(8,128)(2,1)S(1)} %get-tuple-element.628), channel_id=1, source_target_pairs={{0,1},{1,2},{2,3},{3,4},{4,5},{5,6},{6,7},{7,8},{8,9},{9,10},{10,1... | collective-permute-start | bytes 196616 | tf_op jit(solution)/shard_map/while/body/eval_jaxpr/ppermute | solution.py:72
  273.1 8.2 %collective-permute-start.3 = (bf16[1,256,1,128]{3,1,2,0:T(8,128)(2,1)S(1)}, bf16[1,256,1,128]{3,1,2,0:T(8,128)(2,1)S(1)}, u32[]{:S(2)}, u32[]{:S(2)}) collective-permute-start(bf16[1,256,1,128]{3,1,2,0:T(8,128)(2,1)S(1)} %get-tuple-element.629), channel_id=1, source_target_pairs={{0,1},{1,2},{2,3},{3,4},{4,5},{5,6},{6,7},{7,8},{8,9},{9,10},{10,1... | collective-permute-start | bytes 196616 | tf_op jit(solution)/shard_map/while/body/eval_jaxpr/ppermute | solution.py:72
  277.0 6.5 %collective-permute-start.5 = (f32[1,256,1,128]{3,1,2,0:T(8,128)S(1)}, f32[1,256,1,128]{3,1,2,0:T(8,128)S(1)}, u32[]{:S(2)}, u32[]{:S(2)}) collective-permute-start(f32[1,256,1,128]{3,1,2,0:T(8,128)S(1)} %get-tuple-element.631), channel_id=1, source_target_pairs={{0,1},{1,2},{2,3},{3,4},{4,5},{5,6},{6,7},{7,8},{8,9},{9,10},{10,1... | collective-permute-start | bytes 393224 | tf_op jit(solution)/shard_map/while/body/eval_jaxpr/ppermute | solution.py:72
  283.8 8.9 %collective-permute-start.2 = (bf16[1,256,1,128]{3,1,2,0:T(8,128)(2,1)S(1)}, bf16[1,256,1,128]{3,1,2,0:T(8,128)(2,1)S(1)}, u32[]{:S(2)}, u32[]{:S(2)}) collective-permute-start(bf16[1,256,1,128]{3,1,2,0:T(8,128)(2,1)S(1)} %get-tuple-element.628), channel_id=1, source_target_pairs={{0,1},{1,2},{2,3},{3,4},{4,5},{5,6},{6,7},{7,8},{8,9},{9,10},{10,1... | collective-permute-start | bytes 196616 | tf_op jit(solution)/shard_map/while/body/eval_jaxpr/ppermute | solution.py:72
  284.9 8.2 %collective-permute-start.3 = (bf16[1,256,1,128]{3,1,2,0:T(8,128)(2,1)S(1)}, bf16[1,256,1,128]{3,1,2,0:T(8,128)(2,1)S(1)}, u32[]{:S(2)}, u32[]{:S(2)}) collective-permute-start(bf16[1,256,1,128]{3,1,2,0:T(8,128)(2,1)S(1)} %get-tuple-element.629), channel_id=1, source_target_pairs={{0,1},{1,2},{2,3},{3,4},{4,5},{5,6},{6,7},{7,8},{8,9},{9,10},{10,1... | collective-permute-start | bytes 196616 | tf_op jit(solution)/shard_map/while/body/eval_jaxpr/ppermute | solution.py:72
  288.8 6.5 %collective-permute-start.5 = (f32[1,256,1,128]{3,1,2,0:T(8,128)S(1)}, f32[1,256,1,128]{3,1,2,0:T(8,128)S(1)}, u32[]{:S(2)}, u32[]{:S(2)}) collective-permute-start(f32[1,256,1,128]{3,1,2,0:T(8,128)S(1)} %get-tuple-element.631), channel_id=1, source_target_pairs={{0,1},{1,2},{2,3},{3,4},{4,5},{5,6},{6,7},{7,8},{8,9},{9,10},{10,1... | collective-permute-start | bytes 393224 | tf_op jit(solution)/shard_map/while/body/eval_jaxpr/ppermute | solution.py:72
  295.6 8.9 %collective-permute-start.2 = (bf16[1,256,1,128]{3,1,2,0:T(8,128)(2,1)S(1)}, bf16[1,256,1,128]{3,1,2,0:T(8,128)(2,1)S(1)}, u32[]{:S(2)}, u32[]{:S(2)}) collective-permute-start(bf16[1,256,1,128]{3,1,2,0:T(8,128)(2,1)S(1)} %get-tuple-element.628), channel_id=1, source_target_pairs={{0,1},{1,2},{2,3},{3,4},{4,5},{5,6},{6,7},{7,8},{8,9},{9,10},{10,1... | collective-permute-start | bytes 196616 | tf_op jit(solution)/shard_map/while/body/eval_jaxpr/ppermute | solution.py:72
  296.7 8.2 %collective-permute-start.3 = (bf16[1,256,1,128]{3,1,2,0:T(8,128)(2,1)S(1)}, bf16[1,256,1,128]{3,1,2,0:T(8,128)(2,1)S(1)}, u32[]{:S(2)}, u32[]{:S(2)}) collective-permute-start(bf16[1,256,1,128]{3,1,2,0:T(8,128)(2,1)S(1)} %get-tuple-element.629), channel_id=1, source_target_pairs={{0,1},{1,2},{2,3},{3,4},{4,5},{5,6},{6,7},{7,8},{8,9},{9,10},{10,1... | collective-permute-start | bytes 196616 | tf_op jit(solution)/shard_map/while/body/eval_jaxpr/ppermute | solution.py:72
  307.4 8.9 %collective-permute-start.2 = (bf16[1,256,1,128]{3,1,2,0:T(8,128)(2,1)S(1)}, bf16[1,256,1,128]{3,1,2,0:T(8,128)(2,1)S(1)}, u32[]{:S(2)}, u32[]{:S(2)}) collective-permute-start(bf16[1,256,1,128]{3,1,2,0:T(8,128)(2,1)S(1)} %get-tuple-element.628), channel_id=1, source_target_pairs={{0,1},{1,2},{2,3},{3,4},{4,5},{5,6},{6,7},{7,8},{8,9},{9,10},{10,1... | collective-permute-start | bytes 196616 | tf_op jit(solution)/shard_map/while/body/eval_jaxpr/ppermute | solution.py:72
  308.5 8.2 %collective-permute-start.3 = (bf16[1,256,1,128]{3,1,2,0:T(8,128)(2,1)S(1)}, bf16[1,256,1,128]{3,1,2,0:T(8,128)(2,1)S(1)}, u32[]{:S(2)}, u32[]{:S(2)}) collective-permute-start(bf16[1,256,1,128]{3,1,2,0:T(8,128)(2,1)S(1)} %get-tuple-element.629), channel_id=1, source_target_pairs={{0,1},{1,2},{2,3},{3,4},{4,5},{5,6},{6,7},{7,8},{8,9},{9,10},{10,1... | collective-permute-start | bytes 196616 | tf_op jit(solution)/shard_map/while/body/eval_jaxpr/ppermute | solution.py:72
  312.3 6.5 %collective-permute-start.5 = (f32[1,256,1,128]{3,1,2,0:T(8,128)S(1)}, f32[1,256,1,128]{3,1,2,0:T(8,128)S(1)}, u32[]{:S(2)}, u32[]{:S(2)}) collective-permute-start(f32[1,256,1,128]{3,1,2,0:T(8,128)S(1)} %get-tuple-element.631), channel_id=1, source_target_pairs={{0,1},{1,2},{2,3},{3,4},{4,5},{5,6},{6,7},{7,8},{8,9},{9,10},{10,1... | collective-permute-start | bytes 393224 | tf_op jit(solution)/shard_map/while/body/eval_jaxpr/ppermute | solution.py:72
  319.2 67.4 %collective-permute-start.6 = (bf16[1,256,1,128]{3,1,2,0:T(8,128)(2,1)S(1)}, bf16[1,256,1,128]{3,1,2,0:T(8,128)(2,1)S(1)}, u32[]{:S(2)}, u32[]{:S(2)}) collective-permute-start(bf16[1,256,1,128]{3,1,2,0:T(8,128)(2,1)S(1)} %convert.15), channel_id=1, source_target_pairs={{0,112},{1,113},{2,114},{3,115},{4,116},{5,117},{6,118},{7,119},{8... | collective-permute-start | bytes 196616 | tf_op jit(solution)/shard_map/ppermute | solution.py:78
  384.7 6.7 %collective-permute-start.7 = (bf16[1,256,1,128]{3,1,2,0:T(8,128)(2,1)S(1)}, bf16[1,256,1,128]{3,1,2,0:T(8,128)(2,1)S(1)}, u32[]{:S(2)}, u32[]{:S(2)}) collective-permute-start(bf16[1,256,1,128]{3,1,2,0:T(8,128)(2,1)S(1)} %convert.16), channel_id=1, source_target_pairs={{0,112},{1,113},{2,114},{3,115},{4,116},{5,117},{6,118},{7,119},{8... | collective-permute-start | bytes 196616 | tf_op jit(solution)/shard_map/ppermute | solution.py:78
  (58 other events, 321.8 us)
where the time goes:
time: 393 us
  starting transfers between devices  216 us (55%)
  waiting for transfers between devices  118 us (30%)
  matrix products  40.8 us (10%)
  other arithmetic  7.34 us (2%)
  local copies, waits for them, and re-layouts  7.08 us (2%)
    ppermute x64, starting transfers between devices, bwd_body(): k_blk, v_blk, dk_run, dv_run = lax.ppermute(travel, 'ctx', shift_perm)  146 us
    ppermute x32, waiting for transfers between devices, fwd_body(): kv_blk = lax.ppermute(kv_blk, 'ctx', shift_perm)  90.6 us
    ppermute x2, starting transfers between devices, local_attn(): dk_home, dv_home = lax.ppermute((dk_acc, dv_acc), 'ctx', home_perm)  65.6 us
    ppermute x64, waiting for transfers between devices, bwd_body(): k_blk, v_blk, dk_run, dv_run = lax.ppermute(travel, 'ctx', shift_perm)  22.2 us
    dot_general x17, matrix products, fwd_update(): jnp.einsum('bhgqk,bkhd->bhgqd', p_blk.astype(jnp.bfloat16), v_blk, prefer...  8.33 us
  transfers between devices with their start and end apart: 98, of which 62 were waited for; matrix products, arithmetic and copies ran while one was open for 9% of the time, Pallas kernels for 0%

commit v1 on v0

v1 whole, which is shorter than its diff:
```python
import functools

import jax
import jax.numpy as jnp
from jax import lax
from jax.experimental import pallas as pl
from jax.experimental.pallas import tpu as pltpu
from jax.sharding import PartitionSpec as P

OWN, Y1, AT, AO, A2, BT, BO, B2, Y2 = 0, 1, 3, 4, 7, 9, 10, 13, 16
PY1, PAT, PAO, PA2, PBT, PBO, PB2, PS = 2, 5, 6, 8, 11, 12, 14, 15
N_SLOT = 17
ROW = 8
N_DEV = 128
CH = 256
NQ = 1024
HD = 128
TILE = 256
NEG_BIG = -1e30
LOG2E = 1.4426950408889634
SCALE = HD ** -0.5
F32 = jnp.float32
BF16 = jnp.bfloat16


def dot(a, b):
    return lax.dot_general(a, b, (((1,), (0,)), ((), ())), preferred_element_type=F32)


def kernel(q_hbm, k_hbm, v_hbm, do_hbm, o_hbm, dq_hbm, dk_hbm, dv_hbm,
           kv, q_s, do_s, qt_s, dot_s, p_buf, dp_buf, mh, m_s, l_s, d_s, ot_s, dqt_s, part,
           dr, rx, o_s, dq_s, dkv_s,
           lsem, fs, fr, bs, br):
    me = lax.axis_index('ctx')
    core = lax.rem(me, 2)
    x = lax.rem(lax.div(me, 2), 4)
    odd = lax.rem(x, 2)
    base = me - 2 * x
    x_left = lax.rem(x + 3, 4)
    x_right = lax.rem(x + 1, 4)
    x_f = x_left + odd * (x_right - x_left)
    x_g = x_right + odd * (x_left - x_right)
    x_2 = lax.rem(x + 2, 4)
    dev_f = base + 2 * x_f
    dev_g = base + 2 * x_g
    partner = me + 1 - 2 * core
    up = lax.rem(me + ROW, N_DEV)
    down = lax.rem(me + N_DEV - ROW, N_DEV)

    def dev(d):
        return {'dp': 0, 'ctx': d}

    loads = [
        pltpu.make_async_copy(k_hbm, kv.at[OWN, 0], lsem.at[0]),
        pltpu.make_async_copy(v_hbm, kv.at[OWN, 1], lsem.at[1]),
        pltpu.make_async_copy(q_hbm, q_s, lsem.at[2]),
        pltpu.make_async_copy(do_hbm, do_s, lsem.at[3]),
    ]
    for c in loads:
        c.start()

    barrier = pltpu.get_barrier_semaphore()
    peers = (partner, dev_f, dev_g, up, down)
    for d in peers:
        pl.semaphore_signal(barrier, inc=1, device_id=dev(d), device_id_type=pl.DeviceIdType.MESH)
    pl.semaphore_wait(barrier, len(peers))

    def kv_copy(msg, src, dst, d, j):
        return pltpu.make_async_remote_copy(
            src_ref=kv.at[src, j], dst_ref=kv.at[dst, j], send_sem=fs.at[msg, j], recv_sem=fr.at[dst, j],
            device_id=dev(d), device_id_type=pl.DeviceIdType.MESH)

    def kv_wait(slot, j):
        kv_copy(0, slot, slot, partner, j).wait_recv()

    def kv_send(msg, src, dst, d):
        for j in range(2):
            kv_copy(msg, src, dst, d, j).start()

    M_Y1, M_Y2, M_AT, M_AO, M_A2, M_BT, M_BO, M_B2 = range(8)
    M_P = {PY1: 8, PAT: 9, PAO: 10, PA2: 11, PBT: 12, PBO: 13, PB2: 14, PS: 15}

    def to_partner(src, dst):
        kv_send(M_P[dst], src, dst, partner)

    loads[0].wait()
    loads[1].wait()
    kv_send(M_Y1, OWN, Y1, up)

    @pl.when(x_g > x)
    def _():
        kv_send(M_BT, OWN, BT, dev_g)

    @pl.when(x_f > x)
    def _():
        kv_send(M_BO, OWN, BO, dev_f)

    @pl.when(core == 0)
    def _():
        to_partner(OWN, PS)

    loads[2].wait()
    loads[3].wait()
    for t in range(NQ // TILE):
        rows = pl.ds(t * TILE, TILE)
        qt_s[:, rows] = q_s[rows, :].T
        dot_s[:, rows] = do_s[rows, :].T
    m_s[...] = jnp.full_like(m_s, NEG_BIG)
    l_s[...] = jnp.zeros_like(l_s)
    ot_s[...] = jnp.zeros_like(ot_s)
    dqt_s[...] = jnp.zeros_like(dqt_s)

    def fwd_compute(slot, step_id, kind):
        kb = kv[slot, 0]
        vb = kv[slot, 1]
        vt = vb.T
        valid = me >= step_id
        hide = jnp.where(valid, 0.0, -NEG_BIG).astype(F32)
        for t in range(NQ // TILE):
            ls = pl.ds(t * TILE, TILE)
            s = dot(kb, qt_s[:, ls])
            if kind is not None:
                key = lax.broadcasted_iota(jnp.int32, (CH, TILE), 0)
                tok = lax.shift_right_logical(lax.broadcasted_iota(jnp.int32, (CH, TILE), 1) + t * TILE, 2)
                keep = key <= tok if kind == 'own' else key > tok
                s = jnp.where(keep, s, NEG_BIG)
            cm = jnp.max(s, axis=0, keepdims=True) * (SCALE * LOG2E)
            m_old = m_s[:, ls]
            m_new = jnp.maximum(m_old, cm - hide)
            p = jnp.exp2(s * (SCALE * LOG2E) - (m_new + hide))
            p_buf[slot, :, ls] = p
            alpha = jnp.exp2(m_old - m_new)
            m_s[:, ls] = m_new
            mh[slot, :, ls] = m_new
            l_s[:, ls] = l_s[:, ls] * alpha + jnp.sum(p, axis=0, keepdims=True)
            ot_s[:, ls] = ot_s[:, ls] * alpha + dot(vt, p.astype(BF16))
            dp_buf[slot, :, ls] = dot(vb, dot_s[:, ls])

    fwd_compute(OWN, 0, 'own')

    d_f, d_g, d_2 = x - x_f, x - x_g, x - x_2

    def wrap8(d):
        return d + 8 * (d < 0).astype(jnp.int32)

    def chip_dist(i):
        table = {Y1: 4, PY1: 4, AT: 4 + d_f, AO: 4 + d_g, PAT: 4 + d_f, PAO: 4 + d_g, A2: 4 + d_2, PA2: 4 + d_2,
                 BT: wrap8(d_g), BO: wrap8(d_f), PBT: wrap8(d_g), PBO: wrap8(d_f), B2: wrap8(d_2), PB2: wrap8(d_2),
                 PS: 8 * (1 - core)}
        d = 0
        for slot, dist in table.items():
            d = d + (i == slot).astype(jnp.int32) * dist
        return d

    def is_partner(i):
        f = 0
        for slot in M_P:
            f = f + (i == slot).astype(jnp.int32)
        return f

    def fwd_body(i, carry):
        kv_wait(i, 0)
        kv_wait(i, 1)

        @pl.when(i == Y1)
        def _():
            kv_send(M_Y2, Y1, Y2, up)
            kv_send(M_AT, Y1, AT, dev_f)
            kv_send(M_AO, Y1, AO, dev_g)
            to_partner(Y1, PY1)

        @pl.when(i == AT)
        def _():
            to_partner(AT, PAT)

        @pl.when(i == AO)
        def _():
            kv_send(M_A2, AO, A2, dev_f)
            to_partner(AO, PAO)
            kv_wait(Y2, 0)
            kv_wait(Y2, 1)

            @pl.when(x_g < x)
            def _():
                kv_send(M_BT, Y2, BT, dev_g)

            @pl.when(x_f < x)
            def _():
                kv_send(M_BO, Y2, BO, dev_f)

            @pl.when(core == 1)
            def _():
                to_partner(Y2, PS)

        @pl.when(i == A2)
        def _():
            to_partner(A2, PA2)

        @pl.when(i == BT)
        def _():
            to_partner(BT, PBT)

        @pl.when(i == BO)
        def _():
            kv_send(M_B2, BO, B2, dev_g)
            to_partner(BO, PBO)

        @pl.when(i == B2)
        def _():
            to_partner(B2, PB2)

        step_id = 2 * chip_dist(i) + is_partner(i) * (2 * core - 1)
        fwd_compute(i, step_id, None)
        return carry

    lax.fori_loop(1, N_SLOT - 1, fwd_body, 0)
    fwd_compute(Y2, 16, 'far')

    for t in range(NQ // TILE):
        ls = pl.ds(t * TILE, TILE)
        rl = 1.0 / l_s[:, ls]
        l_s[:, ls] = rl
        ot = ot_s[:, ls] * rl
        d_s[:, ls] = jnp.sum(ot * dot_s[:, ls].astype(F32), axis=0, keepdims=True)
        o_s[ls, :] = ot.T.astype(BF16)
    o_out = pltpu.make_async_copy(o_s, o_hbm, lsem.at[4])
    o_out.start()

    def part_copy(msg, src, dst_ref, d, j, sem):
        return pltpu.make_async_remote_copy(
            src_ref=part.at[src, j], dst_ref=dst_ref, send_sem=bs.at[msg, j], recv_sem=br.at[sem, j],
            device_id=dev(d), device_id_type=pl.DeviceIdType.MESH)

    R_A2, R_B2, R_AT, R_AO, R_BT, R_BO, R_Y2, R_YA = range(8)

    def give(src, n):
        for j in (1, 0):
            part_copy(n, src, dr.at[n, j], partner, j, n).start()

    def got(n, j):
        part_copy(n, 0, dr.at[n, j], partner, j, n).wait_recv()

    def send(src, n, d, j):
        part_copy(8 + n, src, rx.at[n, j], d, j, 8 + n).start()

    def recv(n, j):
        part_copy(8 + n, 0, rx.at[n, j], partner, j, 8 + n).wait_recv()

    D_SLOT = {PY1: 0, PAT: 1, PAO: 2, PA2: 3, PBT: 4, PBO: 5, PB2: 6, PS: 7}

    def merge_send(slot, n_d, n_r, d):
        for j in (1, 0):
            got(n_d, j)
            part[slot, j] += dr[n_d, j]
            send(slot, n_r, d, j)

    def bwd_body(t0, carry):
        i = N_SLOT - 1 - t0
        kb = kv[i, 0]
        kt = kb.T
        dk = jnp.zeros((CH, HD), F32)
        dv = jnp.zeros((CH, HD), F32)
        for t in range(NQ // TILE):
            ls = pl.ds(t * TILE, TILE)
            f = jnp.exp2(mh[i, :, ls] - m_s[:, ls]) * l_s[:, ls]
            p = p_buf[i, :, ls] * f
            dv = dv + dot(p.astype(BF16), do_s[ls, :])
            ds = (p * (dp_buf[i, :, ls] - d_s[:, ls])).astype(BF16)
            dk = dk + dot(ds, q_s[ls, :])
            dqt_s[:, ls] += dot(kt, ds)
        part[i, 0] = dk * SCALE
        part[i, 1] = dv

        for slot, n in D_SLOT.items():
            @pl.when(i == slot)
            def _(slot=slot, n=n):
                give(slot, n)

        @pl.when(i == B2)
        def _():
            merge_send(B2, 6, R_B2, dev_g)

        @pl.when(i == BT)
        def _():
            merge_send(BT, 4, R_BT, dev_g)

        @pl.when(i == A2)
        def _():
            merge_send(A2, 3, R_A2, dev_f)

        @pl.when(i == AT)
        def _():
            merge_send(AT, 1, R_AT, dev_f)

        return carry

    lax.fori_loop(0, N_SLOT, bwd_body, 0)

    def relay(slot, n_d, n_in, n_out, d):
        for j in (1, 0):
            got(n_d, j)
            recv(n_in, j)
            part[slot, j] += dr[n_d, j] + rx[n_in, j]
            send(slot, n_out, d, j)

    relay(BO, 5, R_B2, R_BO, dev_f)
    relay(AO, 2, R_A2, R_AO, dev_g)

    for t in range(NQ // TILE):
        ls = pl.ds(t * TILE, TILE)
        dq_s[ls, :] = (dqt_s[:, ls] * SCALE).T.astype(BF16)
    dq_out = pltpu.make_async_copy(dq_s, dq_hbm, lsem.at[5])
    dq_out.start()

    def home_or_far(far):
        return far.astype(jnp.int32) * Y2

    for j in (1, 0):
        got(0, j)
        part[Y1, j] += dr[0, j]
        got(7, j)
        part[core * Y2, j] += dr[7, j]
    for j in (1, 0):
        recv(R_BT, j)
        part[home_or_far(x_g < x), j] += rx[R_BT, j]
        recv(R_BO, j)
        part[home_or_far(x_f < x), j] += rx[R_BO, j]
        send(Y2, R_Y2, down, j)
    for j in (1, 0):
        recv(R_AT, j)
        recv(R_AO, j)
        part[Y1, j] += rx[R_AT, j] + rx[R_AO, j]
    for j in (1, 0):
        recv(R_Y2, j)
        part[Y1, j] += rx[R_Y2, j]
        send(Y1, R_YA, down, j)
    outs = []
    for j, hbm in ((1, dv_hbm), (0, dk_hbm)):
        recv(R_YA, j)
        dkv_s[j] = (part[OWN, j] + rx[R_YA, j]).astype(BF16)
        c = pltpu.make_async_copy(dkv_s.at[j], hbm, lsem.at[6 + j])
        c.start()
        outs.append(c)

    for msg in range(16):
        for j in range(2):
            kv_copy(msg, 0, 0, partner, j).wait_send()
            part_copy(msg, 0, dr.at[0, j], partner, j, 0).wait_send()
    o_out.wait()
    dq_out.wait()
    for c in outs:
        c.wait()


def solution(mesh):
    seq_spec = P('dp', 'ctx', None, None)

    def local_attn(q_loc, k_loc, v_loc, do_loc):
        q = q_loc.reshape(NQ, HD)
        do = do_loc.reshape(NQ, HD)
        k = k_loc.reshape(CH, HD)
        v = v_loc.reshape(CH, HD)
        anyspec = pl.BlockSpec(memory_space=pl.ANY)
        o, dq, dk, dv = pl.pallas_call(
            kernel,
            out_shape=(jax.ShapeDtypeStruct((NQ, HD), BF16), jax.ShapeDtypeStruct((NQ, HD), BF16),
                       jax.ShapeDtypeStruct((CH, HD), BF16), jax.ShapeDtypeStruct((CH, HD), BF16)),
            in_specs=[anyspec] * 4,
            out_specs=[anyspec] * 4,
            scratch_shapes=[
                pltpu.VMEM((N_SLOT, 2, CH, HD), BF16),
                pltpu.VMEM((NQ, HD), BF16),
                pltpu.VMEM((NQ, HD), BF16),
                pltpu.VMEM((HD, NQ), BF16),
                pltpu.VMEM((HD, NQ), BF16),
                pltpu.VMEM((N_SLOT, CH, NQ), F32),
                pltpu.VMEM((N_SLOT, CH, NQ), F32),
                pltpu.VMEM((N_SLOT, 1, NQ), F32),
                pltpu.VMEM((1, NQ), F32),
                pltpu.VMEM((1, NQ), F32),
                pltpu.VMEM((1, NQ), F32),
                pltpu.VMEM((HD, NQ), F32),
                pltpu.VMEM((HD, NQ), F32),
                pltpu.VMEM((N_SLOT, 2, CH, HD), F32),
                pltpu.VMEM((8, 2, CH, HD), F32),
                pltpu.VMEM((8, 2, CH, HD), F32),
                pltpu.VMEM((NQ, HD), BF16),
                pltpu.VMEM((NQ, HD), BF16),
                pltpu.VMEM((2, CH, HD), BF16),
                pltpu.SemaphoreType.DMA((8,)),
                pltpu.SemaphoreType.DMA((16, 2)),
                pltpu.SemaphoreType.DMA((N_SLOT, 2)),
                pltpu.SemaphoreType.DMA((16, 2)),
                pltpu.SemaphoreType.DMA((16, 2)),
            ],
            compiler_params=pltpu.CompilerParams(
                collective_id=0, has_side_effects=True, vmem_limit_bytes=63 * 1024 * 1024),
            name='swa_fwd_bwd',
        )(q, k, v, do)
        return o.reshape(q_loc.shape), dq.reshape(q_loc.shape), dk.reshape(k_loc.shape), dv.reshape(k_loc.shape)

    return jax.shard_map(local_attn, mesh=mesh, in_specs=(seq_spec,) * 4, out_specs=(seq_spec,) * 4, check_vma=False)
```

time: 393 us -> 77.6 us (0.20)
  the two profiles are of different devices: /device:TPU:16 before, /device:TPU:2 now
where the time goes in v1:
time: 77.6 us; the launch traced here: 77.4 us
  Pallas kernels  72.6 us (94%)
  local copies, waits for them, and re-layouts  4.14 us (5%)
    pallas_call x1, Pallas kernels, local_attn(): pl.pallas_call(kernel, out_shape=(jax.ShapeDtypeStruct((NQ, HD), BF16), j...  72.6 us
    unnamed x10, local copies, waits for them, and re-layouts  4.14 us

profile of v1, /device:TPU:2, one launch (start us, length us, event | category | flops | bytes accessed | tf_op | source)
XLA Modules:
  0.0 77.4 jit_solution(5568252625089498467)
XLA Ops:
  0.6 72.6 %swa_fwd_bwd.1 = (bf16[1024,128]{1,0:T(8,128)(2,1)}, bf16[1024,128]{1,0:T(8,128)(2,1)}, bf16[256,128]{1,0:T(8,128)(2,1)}, bf16[256,128]{1,0:T(8,128)(2,1)}) custom-call(bf16[1024,128]{1,0:T(8,128)(2,1)} %bitcast.8, bf16[256,128]{1,0:T(8,128)(2,1)} %bitcast.12, bf16[256,128]{1,0:T(8,128)(2,1)} %bitcast.13, bf16[1024,128]{1,0:T(8,128)(2,1)} %bitcast.9), custom_call_target="tpu_custom_call" | custom-call | tf_op jit(solution)/shard_map/swa_fwd_bwd/pallas_call | solution.py:364
  73.2 0.0 copy-start
  73.2 1.8 %copy.12 = bf16[1,256,4,128]{3,2,1,0:T(4,128)(2,1)} copy(bf16[1,256,4,128]{3,2,1,0:T(4,128)(2,1)} %bitcast.11) | data formatting | bytes 524288
  75.0 0.0 copy-done
  75.0 0.0 copy-start.2
  75.0 0.7 copy.13
  75.7 0.2 copy-done.2
  75.9 0.0 copy-start.1
  75.9 0.6 copy.14
  76.5 0.2 copy-done.1
  76.7 0.6 copy.15
Async XLA Ops:
  73.2 1.8 %copy-start = (bf16[1024,128]{1,0:T(8,128)(2,1)S(1)}, bf16[1024,128]{1,0:T(8,128)(2,1)}, u32[]{:S(2)}) copy-start(bf16[1024,128]{1,0:T(8,128)(2,1)} %get-tuple-element.9) | copy-start | bytes 786436
  75.0 0.9 %copy-start.2 = (bf16[256,128]{1,0:T(8,128)(2,1)S(1)}, bf16[256,128]{1,0:T(8,128)(2,1)}, u32[]{:S(2)}) copy-start(bf16[256,128]{1,0:T(8,128)(2,1)} %get-tuple-element.10) | copy-start | bytes 196612
  75.9 0.9 %copy-start.1 = (bf16[256,128]{1,0:T(8,128)(2,1)S(1)}, bf16[256,128]{1,0:T(8,128)(2,1)}, u32[]{:S(2)}) copy-start(bf16[256,128]{1,0:T(8,128)(2,1)} %get-tuple-element.11) | copy-start | bytes 196612

commit v2 on v1

--- a/solution.py
+++ b/solution.py
@@ -59,11 +59,24 @@
     for c in loads:
         c.start()
 
+    row = lax.div(me, ROW)
+    has_up = row < N_DEV // ROW - 1
+    e1 = row >= 1
+    e2 = row >= 2
+    e_bt = jnp.logical_or(x_g < x, e2)
+    e_bo = jnp.logical_or(x_f < x, e2)
+    e_b2 = jnp.logical_or(x_2 < x, e2)
+
     barrier = pltpu.get_barrier_semaphore()
-    peers = (partner, dev_f, dev_g, up, down)
-    for d in peers:
+
+    def greet(d):
         pl.semaphore_signal(barrier, inc=1, device_id=dev(d), device_id_type=pl.DeviceIdType.MESH)
-    pl.semaphore_wait(barrier, len(peers))
+
+    pl.when(has_up)(lambda: greet(up))
+    pl.when(e1)(lambda: greet(down))
+    for d in (dev_f, dev_g, partner):
+        greet(d)
+    pl.semaphore_wait(barrier, 3 + has_up.astype(jnp.int32) + e1.astype(jnp.int32))
 
     def kv_copy(msg, src, dst, d, j):
         return pltpu.make_async_remote_copy(
@@ -73,31 +86,21 @@
     def kv_wait(slot, j):
         kv_copy(0, slot, slot, partner, j).wait_recv()
 
-    def kv_send(msg, src, dst, d):
-        for j in range(2):
-            kv_copy(msg, src, dst, d, j).start()
+    def kv_send(msg, src, dst, d, j):
+        kv_copy(msg, src, dst, d, j).start()
 
     M_Y1, M_Y2, M_AT, M_AO, M_A2, M_BT, M_BO, M_B2 = range(8)
     M_P = {PY1: 8, PAT: 9, PAO: 10, PA2: 11, PBT: 12, PBO: 13, PB2: 14, PS: 15}
 
-    def to_partner(src, dst):
-        kv_send(M_P[dst], src, dst, partner)
-
-    loads[0].wait()
-    loads[1].wait()
-    kv_send(M_Y1, OWN, Y1, up)
-
-    @pl.when(x_g > x)
-    def _():
-        kv_send(M_BT, OWN, BT, dev_g)
-
-    @pl.when(x_f > x)
-    def _():
-        kv_send(M_BO, OWN, BO, dev_f)
-
-    @pl.when(core == 0)
-    def _():
-        to_partner(OWN, PS)
+    def to_partner(src, dst, j):
+        kv_send(M_P[dst], src, dst, partner, j)
+
+    for j in range(2):
+        loads[j].wait()
+        pl.when(has_up)(lambda: kv_send(M_Y1, OWN, Y1, up, j))
+        pl.when(x_g > x)(lambda: kv_send(M_BT, OWN, BT, dev_g, j))
+        pl.when(x_f > x)(lambda: kv_send(M_BO, OWN, BO, dev_f, j))
+        pl.when(core == 0)(lambda: to_partner(OWN, PS, j))
 
     loads[2].wait()
     loads[3].wait()
@@ -110,12 +113,10 @@
     ot_s[...] = jnp.zeros_like(ot_s)
     dqt_s[...] = jnp.zeros_like(dqt_s)
 
-    def fwd_compute(slot, step_id, kind):
+    def fwd_compute(slot, kind):
         kb = kv[slot, 0]
         vb = kv[slot, 1]
         vt = vb.T
-        valid = me >= step_id
-        hide = jnp.where(valid, 0.0, -NEG_BIG).astype(F32)
         for t in range(NQ // TILE):
             ls = pl.ds(t * TILE, TILE)
             s = dot(kb, qt_s[:, ls])
@@ -126,8 +127,8 @@
                 s = jnp.where(keep, s, NEG_BIG)
             cm = jnp.max(s, axis=0, keepdims=True) * (SCALE * LOG2E)
             m_old = m_s[:, ls]
-            m_new = jnp.maximum(m_old, cm - hide)
-            p = jnp.exp2(s * (SCALE * LOG2E) - (m_new + hide))
+            m_new = jnp.maximum(m_old, cm)
+            p = jnp.exp2(s * (SCALE * LOG2E) - m_new)
             p_buf[slot, :, ls] = p
             alpha = jnp.exp2(m_old - m_new)
             m_s[:, ls] = m_new
@@ -136,85 +137,87 @@
             ot_s[:, ls] = ot_s[:, ls] * alpha + dot(vt, p.astype(BF16))
             dp_buf[slot, :, ls] = dot(vb, dot_s[:, ls])
 
-    fwd_compute(OWN, 0, 'own')
-
-    d_f, d_g, d_2 = x - x_f, x - x_g, x - x_2
-
-    def wrap8(d):
-        return d + 8 * (d < 0).astype(jnp.int32)
-
-    def chip_dist(i):
-        table = {Y1: 4, PY1: 4, AT: 4 + d_f, AO: 4 + d_g, PAT: 4 + d_f, PAO: 4 + d_g, A2: 4 + d_2, PA2: 4 + d_2,
-                 BT: wrap8(d_g), BO: wrap8(d_f), PBT: wrap8(d_g), PBO: wrap8(d_f), B2: wrap8(d_2), PB2: wrap8(d_2),
-                 PS: 8 * (1 - core)}
-        d = 0
-        for slot, dist in table.items():
-            d = d + (i == slot).astype(jnp.int32) * dist
-        return d
-
-    def is_partner(i):
-        f = 0
-        for slot in M_P:
-            f = f + (i == slot).astype(jnp.int32)
-        return f
+    fwd_compute(OWN, 'own')
+
+    def here(i):
+        n = jnp.int32(0)
+        for slots, e in (((Y1, PY1, AT, AO, PAT, PAO, A2, PA2), e1), ((BT, PBT), e_bt), ((BO, PBO), e_bo),
+                         ((B2, PB2), e_b2), ((PS,), jnp.logical_or(core == 1, e2)), ((OWN,), row >= 0), ((Y2,), e2)):
+            for slot in slots:
+                n = n + (i == slot).astype(jnp.int32) * e.astype(jnp.int32)
+        return n > 0
 
     def fwd_body(i, carry):
-        kv_wait(i, 0)
-        kv_wait(i, 1)
-
-        @pl.when(i == Y1)
-        def _():
-            kv_send(M_Y2, Y1, Y2, up)
-            kv_send(M_AT, Y1, AT, dev_f)
-            kv_send(M_AO, Y1, AO, dev_g)
-            to_partner(Y1, PY1)
-
-        @pl.when(i == AT)
-        def _():
-            to_partner(AT, PAT)
-
-        @pl.when(i == AO)
-        def _():
-            kv_send(M_A2, AO, A2, dev_f)
-            to_partner(AO, PAO)
-            kv_wait(Y2, 0)
-            kv_wait(Y2, 1)
-
-            @pl.when(x_g < x)
+        @pl.when(here(i))
+        def _():
+            @pl.when(i == Y1)
             def _():
-                kv_send(M_BT, Y2, BT, dev_g)
-
-            @pl.when(x_f < x)
+                for j in range(2):
+                    kv_wait(Y1, j)
+                    pl.when(has_up)(lambda: kv_send(M_Y2, Y1, Y2, up, j))
+                    kv_send(M_AT, Y1, AT, dev_f, j)
+                    kv_send(M_AO, Y1, AO, dev_g, j)
+                    to_partner(Y1, PY1, j)
+
+            @pl.when(i == AT)
             def _():
-                kv_send(M_BO, Y2, BO, dev_f)
-
-            @pl.when(core == 1)
+                for j in range(2):
+                    kv_wait(AO, j)
+                    kv_send(M_A2, AO, A2, dev_f, j)
+                    to_partner(AO, PAO, j)
+
+                    @pl.when(e2)
+                    def _():
+                        kv_wait(Y2, j)
+                        pl.when(x_g < x)(lambda: kv_send(M_BT, Y2, BT, dev_g, j))
+                        pl.when(x_f < x)(lambda: kv_send(M_BO, Y2, BO, dev_f, j))
+                        pl.when(core == 1)(lambda: to_partner(Y2, PS, j))
+
+                    kv_wait(AT, j)
+                    to_partner(AT, PAT, j)
+
+            is_p = jnp.int32(0)
+            for slot in M_P:
+                is_p = is_p + (i == slot).astype(jnp.int32)
+
+            @pl.when(is_p > 0)
             def _():
-                to_partner(Y2, PS)
-
-        @pl.when(i == A2)
-        def _():
-            to_partner(A2, PA2)
-
-        @pl.when(i == BT)
-        def _():
-            to_partner(BT, PBT)
+                kv_wait(i, 0)
+                kv_wait(i, 1)
+
+            fwd_compute(i, None)
+
+        @pl.when(i == PAO)
+        def _():
+            for j in range(2):
+                @pl.when(e_bo)
+                def _():
+                    kv_wait(BO, j)
+                    kv_send(M_B2, BO, B2, dev_g, j)
+                    to_partner(BO, PBO, j)
+
+                @pl.when(e1)
+                def _():
+                    kv_wait(A2, j)
+                    to_partner(A2, PA2, j)
+
+                @pl.when(e_bt)
+                def _():
+                    kv_wait(BT, j)
+                    to_partner(BT, PBT, j)
 
         @pl.when(i == BO)
         def _():
-            kv_send(M_B2, BO, B2, dev_g)
-            to_partner(BO, PBO)
-
-        @pl.when(i == B2)
-        def _():
-            to_partner(B2, PB2)
-
-        step_id = 2 * chip_dist(i) + is_partner(i) * (2 * core - 1)
-        fwd_compute(i, step_id, None)
+            @pl.when(e_b2)
+            def _():
+                for j in range(2):
+                    kv_wait(B2, j)
+                    to_partner(B2, PB2, j)
+
         return carry
 
     lax.fori_loop(1, N_SLOT - 1, fwd_body, 0)
-    fwd_compute(Y2, 16, 'far')
+    pl.when(e2)(lambda: fwd_compute(Y2, 'far'))
 
     for t in range(NQ // TILE):
         ls = pl.ds(t * TILE, TILE)
@@ -254,8 +257,7 @@
             part[slot, j] += dr[n_d, j]
             send(slot, n_r, d, j)
 
-    def bwd_body(t0, carry):
-        i = N_SLOT - 1 - t0
+    def bwd_compute(i):
         kb = kv[i, 0]
         kt = kb.T
         dk = jnp.zeros((CH, HD), F32)
@@ -292,9 +294,15 @@
         def _():
             merge_send(AT, 1, R_AT, dev_f)
 
+    def bwd_body(t0, carry):
+        i = N_SLOT - 1 - t0
+        pl.when(here(i))(lambda: bwd_compute(i))
+
+        @pl.when(jnp.logical_and(i == AO, e_bo))
+        def _():
+            relay(BO, 5, R_B2, R_BO, dev_f)
+
         return carry
-
-    lax.fori_loop(0, N_SLOT, bwd_body, 0)
 
     def relay(slot, n_d, n_in, n_out, d):
         for j in (1, 0):
@@ -303,8 +311,8 @@
             part[slot, j] += dr[n_d, j] + rx[n_in, j]
             send(slot, n_out, d, j)
 
-    relay(BO, 5, R_B2, R_BO, dev_f)
-    relay(AO, 2, R_A2, R_AO, dev_g)
+    lax.fori_loop(0, N_SLOT, bwd_body, 0)
+    pl.when(e1)(lambda: relay(AO, 2, R_A2, R_AO, dev_g))
 
     for t in range(NQ // TILE):
         ls = pl.ds(t * TILE, TILE)
@@ -315,37 +323,53 @@
     def home_or_far(far):
         return far.astype(jnp.int32) * Y2
 
+    def add_rx(slot, n, j):
+        recv(n, j)
+        part[slot, j] += rx[n, j]
+
+    r_bt = jnp.logical_or(x < x_g, e2)
+    r_bo = jnp.logical_or(x < x_f, e2)
+    r_ps = jnp.logical_or(core == 0, e2)
+    r_y2 = jnp.logical_and(has_up, e1)
     for j in (1, 0):
-        got(0, j)
-        part[Y1, j] += dr[0, j]
-        got(7, j)
-        part[core * Y2, j] += dr[7, j]
+        @pl.when(r_ps)
+        def _():
+            got(7, j)
+            part[core * Y2, j] += dr[7, j]
+
+        pl.when(r_bt)(lambda: add_rx(home_or_far(x_g < x), R_BT, j))
+        pl.when(r_bo)(lambda: add_rx(home_or_far(x_f < x), R_BO, j))
+        pl.when(e2)(lambda: send(Y2, R_Y2, down, j))
     for j in (1, 0):
-        recv(R_BT, j)
-        part[home_or_far(x_g < x), j] += rx[R_BT, j]
-        recv(R_BO, j)
-        part[home_or_far(x_f < x), j] += rx[R_BO, j]
-        send(Y2, R_Y2, down, j)
-    for j in (1, 0):
-        recv(R_AT, j)
-        recv(R_AO, j)
-        part[Y1, j] += rx[R_AT, j] + rx[R_AO, j]
-    for j in (1, 0):
-        recv(R_Y2, j)
-        part[Y1, j] += rx[R_Y2, j]
-        send(Y1, R_YA, down, j)
+        @pl.when(e1)
+        def _():
+            got(0, j)
+            part[Y1, j] += dr[0, j]
+            add_rx(Y1, R_AT, j)
+            add_rx(Y1, R_AO, j)
+            pl.when(has_up)(lambda: add_rx(Y1, R_Y2, j))
+            send(Y1, R_YA, down, j)
     outs = []
     for j, hbm in ((1, dv_hbm), (0, dk_hbm)):
-        recv(R_YA, j)
-        dkv_s[j] = (part[OWN, j] + rx[R_YA, j]).astype(BF16)
+        pl.when(has_up)(lambda: add_rx(OWN, R_YA, j))
+        dkv_s[j] = part[OWN, j].astype(BF16)
         c = pltpu.make_async_copy(dkv_s.at[j], hbm, lsem.at[6 + j])
         c.start()
         outs.append(c)
 
-    for msg in range(16):
-        for j in range(2):
-            kv_copy(msg, 0, 0, partner, j).wait_send()
-            part_copy(msg, 0, dr.at[0, j], partner, j, 0).wait_send()
+    up1 = jnp.logical_and(has_up, e1)
+    kv_sent = ((M_Y1, has_up), (M_Y2, up1), (M_AT, e1), (M_AO, e1), (M_A2, e1),
+               (M_BT, jnp.logical_or(x_g > x, e2)), (M_BO, jnp.logical_or(x_f > x, e2)), (M_B2, e_bo),
+               (M_P[PY1], e1), (M_P[PAT], e1), (M_P[PAO], e1), (M_P[PA2], e1), (M_P[PBT], e_bt), (M_P[PBO], e_bo),
+               (M_P[PB2], e_b2), (M_P[PS], r_ps))
+    part_sent = ((0, e1), (1, e1), (2, e1), (3, e1), (4, e_bt), (5, e_bo), (6, e_b2), (7, jnp.logical_or(core == 1, e2)),
+                 (8 + R_A2, e1), (8 + R_B2, e_b2), (8 + R_AT, e1), (8 + R_AO, e1), (8 + R_BT, e_bt), (8 + R_BO, e_bo),
+                 (8 + R_Y2, e2), (8 + R_YA, e1))
+    for j in range(2):
+        for msg, e in kv_sent:
+            pl.when(e)(lambda: kv_copy(msg, 0, 0, partner, j).wait_send())
+        for msg, e in part_sent:
+            pl.when(e)(lambda: part_copy(msg, 0, dr.at[0, j], partner, j, 0).wait_send())
     o_out.wait()
     dq_out.wait()
     for c in outs:

time: 77.6 us -> 70.7 us (0.911)
  the two profiles are of different devices: /device:TPU:2 before, /device:TPU:62 now
where the time goes in v2:
time: 70.7 us; the launch traced here: 70.4 us
  Pallas kernels  65.6 us (93%)
  local copies, waits for them, and re-layouts  4.14 us (6%)
    pallas_call x1, Pallas kernels, local_attn(): pl.pallas_call(kernel, out_shape=(jax.ShapeDtypeStruct((NQ, HD), BF16), j...  65.6 us
    unnamed x10, local copies, waits for them, and re-layouts  4.14 us

profile of v2, /device:TPU:62, one launch (start us, length us, event | category | flops | bytes accessed | tf_op | source)
XLA Modules:
  0.0 70.4 jit_solution(9220048406154155530)
XLA Ops:
  0.6 65.6 %swa_fwd_bwd.1 = (bf16[1024,128]{1,0:T(8,128)(2,1)}, bf16[1024,128]{1,0:T(8,128)(2,1)}, bf16[256,128]{1,0:T(8,128)(2,1)}, bf16[256,128]{1,0:T(8,128)(2,1)}) custom-call(bf16[1024,128]{1,0:T(8,128)(2,1)} %bitcast.8, bf16[256,128]{1,0:T(8,128)(2,1)} %bitcast.12, bf16[256,128]{1,0:T(8,128)(2,1)} %bitcast.13, bf16[1024,128]{1,0:T(8,128)(2,1)} %bitcast.9), custom_call_target="tpu_custom_call" | custom-call | tf_op jit(solution)/shard_map/swa_fwd_bwd/pallas_call | solution.py:388
  66.3 0.0 copy-start
  66.3 1.8 %copy.12 = bf16[1,256,4,128]{3,2,1,0:T(4,128)(2,1)} copy(bf16[1,256,4,128]{3,2,1,0:T(4,128)(2,1)} %bitcast.11) | data formatting | bytes 524288
  68.1 0.0 copy-done
  68.1 0.0 copy-start.2
  68.1 0.7 copy.13
  68.8 0.2 copy-done.2
  68.9 0.0 copy-start.1
  68.9 0.6 copy.14
  69.6 0.2 copy-done.1
  69.8 0.6 copy.15
Async XLA Ops:
  66.3 1.8 %copy-start = (bf16[1024,128]{1,0:T(8,128)(2,1)S(1)}, bf16[1024,128]{1,0:T(8,128)(2,1)}, u32[]{:S(2)}) copy-start(bf16[1024,128]{1,0:T(8,128)(2,1)} %get-tuple-element.9) | copy-start | bytes 786436
  68.1 0.9 %copy-start.2 = (bf16[256,128]{1,0:T(8,128)(2,1)S(1)}, bf16[256,128]{1,0:T(8,128)(2,1)}, u32[]{:S(2)}) copy-start(bf16[256,128]{1,0:T(8,128)(2,1)} %get-tuple-element.10) | copy-start | bytes 196612
  68.9 0.9 %copy-start.1 = (bf16[256,128]{1,0:T(8,128)(2,1)S(1)}, bf16[256,128]{1,0:T(8,128)(2,1)}, u32[]{:S(2)}) copy-start(bf16[256,128]{1,0:T(8,128)(2,1)} %get-tuple-element.11) | copy-start | bytes 196612

commit v3 on v2

--- a/solution.py
+++ b/solution.py
@@ -7,8 +7,8 @@
 from jax.experimental.pallas import tpu as pltpu
 from jax.sharding import PartitionSpec as P
 
-OWN, Y1, AT, AO, A2, BT, BO, B2, Y2 = 0, 1, 3, 4, 7, 9, 10, 13, 16
-PY1, PAT, PAO, PA2, PBT, PBO, PB2, PS = 2, 5, 6, 8, 11, 12, 14, 15
+OWN, Y1, AT, AO, A2, BT, BO, B2, Y2 = 0, 1, 3, 4, 7, 10, 11, 14, 16
+PY1, PAT, PAO, PA2, PS, PBT, PBO, PB2 = 2, 5, 6, 8, 9, 12, 13, 15
 N_SLOT = 17
 ROW = 8
 N_DEV = 128
@@ -30,7 +30,7 @@
 def kernel(q_hbm, k_hbm, v_hbm, do_hbm, o_hbm, dq_hbm, dk_hbm, dv_hbm,
            kv, q_s, do_s, qt_s, dot_s, p_buf, dp_buf, mh, m_s, l_s, d_s, ot_s, dqt_s, part,
            dr, rx, o_s, dq_s, dkv_s,
-           lsem, fs, fr, bs, br):
+           al_s, pb_s, lsem, fs, fr, bs, br):
     me = lax.axis_index('ctx')
     core = lax.rem(me, 2)
     x = lax.rem(lax.div(me, 2), 4)
@@ -43,6 +43,7 @@
     x_2 = lax.rem(x + 2, 4)
     dev_f = base + 2 * x_f
     dev_g = base + 2 * x_g
+    dev_2 = base + 2 * x_2
     partner = me + 1 - 2 * core
     up = lax.rem(me + ROW, N_DEV)
     down = lax.rem(me + N_DEV - ROW, N_DEV)
@@ -74,9 +75,9 @@
 
     pl.when(has_up)(lambda: greet(up))
     pl.when(e1)(lambda: greet(down))
-    for d in (dev_f, dev_g, partner):
+    for d in (dev_f, dev_g, dev_2, partner):
         greet(d)
-    pl.semaphore_wait(barrier, 3 + has_up.astype(jnp.int32) + e1.astype(jnp.int32))
+    pl.semaphore_wait(barrier, 4 + has_up.astype(jnp.int32) + e1.astype(jnp.int32))
 
     def kv_copy(msg, src, dst, d, j):
         return pltpu.make_async_remote_copy(
@@ -100,6 +101,7 @@
         pl.when(has_up)(lambda: kv_send(M_Y1, OWN, Y1, up, j))
         pl.when(x_g > x)(lambda: kv_send(M_BT, OWN, BT, dev_g, j))
         pl.when(x_f > x)(lambda: kv_send(M_BO, OWN, BO, dev_f, j))
+        pl.when(x_2 > x)(lambda: kv_send(M_B2, OWN, B2, dev_2, j))
         pl.when(core == 0)(lambda: to_partner(OWN, PS, j))
 
     loads[2].wait()
@@ -125,17 +127,23 @@
                 tok = lax.shift_right_logical(lax.broadcasted_iota(jnp.int32, (CH, TILE), 1) + t * TILE, 2)
                 keep = key <= tok if kind == 'own' else key > tok
                 s = jnp.where(keep, s, NEG_BIG)
-            cm = jnp.max(s, axis=0, keepdims=True) * (SCALE * LOG2E)
+            p_buf[slot, :, ls] = s
+            mh[slot, :, ls] = jnp.maximum(m_s[:, ls], jnp.max(s, axis=0, keepdims=True) * (SCALE * LOG2E))
+        for t in range(NQ // TILE):
+            ls = pl.ds(t * TILE, TILE)
             m_old = m_s[:, ls]
-            m_new = jnp.maximum(m_old, cm)
-            p = jnp.exp2(s * (SCALE * LOG2E) - m_new)
+            m_new = mh[slot, :, ls]
+            p = jnp.exp2(p_buf[slot, :, ls] * (SCALE * LOG2E) - m_new)
             p_buf[slot, :, ls] = p
             alpha = jnp.exp2(m_old - m_new)
             m_s[:, ls] = m_new
-            mh[slot, :, ls] = m_new
             l_s[:, ls] = l_s[:, ls] * alpha + jnp.sum(p, axis=0, keepdims=True)
-            ot_s[:, ls] = ot_s[:, ls] * alpha + dot(vt, p.astype(BF16))
+            al_s[:, ls] = alpha
             dp_buf[slot, :, ls] = dot(vb, dot_s[:, ls])
+            pb_s[:, ls] = p.astype(BF16)
+        for t in range(NQ // TILE):
+            ls = pl.ds(t * TILE, TILE)
+            ot_s[:, ls] = ot_s[:, ls] * al_s[:, ls] + dot(vt, pb_s[:, ls])
 
     fwd_compute(OWN, 'own')
 
@@ -147,7 +155,23 @@
                 n = n + (i == slot).astype(jnp.int32) * e.astype(jnp.int32)
         return n > 0
 
+    def take(slot, partner_slot, e):
+        @pl.when(e)
+        def _():
+            for j in range(2):
+                kv_wait(slot, j)
+                to_partner(slot, partner_slot, j)
+
     def fwd_body(i, carry):
+        @pl.when(jnp.logical_and(i == PY1, x >= 2))
+        def _():
+            for j in range(2):
+                kv_wait(B2, j)
+                pl.when(has_up)(lambda: kv_send(M_B2, B2, A2, up, j))
+                to_partner(B2, PB2, j)
+
+        pl.when(i == PBT)(lambda: take(B2, PB2, jnp.logical_and(x < 2, e2)))
+
         @pl.when(here(i))
         def _():
             @pl.when(i == Y1)
@@ -155,6 +179,7 @@
                 for j in range(2):
                     kv_wait(Y1, j)
                     pl.when(has_up)(lambda: kv_send(M_Y2, Y1, Y2, up, j))
+                    pl.when(x >= 2)(lambda: kv_send(M_A2, Y1, A2, dev_2, j))
                     kv_send(M_AT, Y1, AT, dev_f, j)
                     kv_send(M_AO, Y1, AO, dev_g, j)
                     to_partner(Y1, PY1, j)
@@ -162,8 +187,15 @@
             @pl.when(i == AT)
             def _():
                 for j in range(2):
+                    @pl.when(x < 2)
+                    def _():
+                        kv_wait(A2, j)
+                        pl.when(has_up)(lambda: kv_send(M_A2, A2, B2, up, j))
+                        to_partner(A2, PA2, j)
+
+                    kv_wait(AT, j)
+                    to_partner(AT, PAT, j)
                     kv_wait(AO, j)
-                    kv_send(M_A2, AO, A2, dev_f, j)
                     to_partner(AO, PAO, j)
 
                     @pl.when(e2)
@@ -173,8 +205,13 @@
                         pl.when(x_f < x)(lambda: kv_send(M_BO, Y2, BO, dev_f, j))
                         pl.when(core == 1)(lambda: to_partner(Y2, PS, j))
 
-                    kv_wait(AT, j)
-                    to_partner(AT, PAT, j)
+            @pl.when(i == A2)
+            def _():
+                @pl.when(x >= 2)
+                def _():
+                    for j in range(2):
+                        kv_wait(A2, j)
+                        to_partner(A2, PA2, j)
 
             is_p = jnp.int32(0)
             for slot in M_P:
@@ -187,47 +224,19 @@
 
             fwd_compute(i, None)
 
-        @pl.when(i == PAO)
-        def _():
-            for j in range(2):
-                @pl.when(e_bo)
-                def _():
-                    kv_wait(BO, j)
-                    kv_send(M_B2, BO, B2, dev_g, j)
-                    to_partner(BO, PBO, j)
-
-                @pl.when(e1)
-                def _():
-                    kv_wait(A2, j)
-                    to_partner(A2, PA2, j)
-
-                @pl.when(e_bt)
-                def _():
-                    kv_wait(BT, j)
-                    to_partner(BT, PBT, j)
-
-        @pl.when(i == BO)
-        def _():
-            @pl.when(e_b2)
-            def _():
-                for j in range(2):
-                    kv_wait(B2, j)
-                    to_partner(B2, PB2, j)
-
         return carry
 
-    lax.fori_loop(1, N_SLOT - 1, fwd_body, 0)
+    lax.fori_loop(1, BT, fwd_body, 0)
     pl.when(e2)(lambda: fwd_compute(Y2, 'far'))
+    take(BT, PBT, e_bt)
+    take(BO, PBO, e_bo)
+    lax.fori_loop(BT, N_SLOT - 1, fwd_body, 0)
 
     for t in range(NQ // TILE):
         ls = pl.ds(t * TILE, TILE)
         rl = 1.0 / l_s[:, ls]
         l_s[:, ls] = rl
-        ot = ot_s[:, ls] * rl
-        d_s[:, ls] = jnp.sum(ot * dot_s[:, ls].astype(F32), axis=0, keepdims=True)
-        o_s[ls, :] = ot.T.astype(BF16)
-    o_out = pltpu.make_async_copy(o_s, o_hbm, lsem.at[4])
-    o_out.start()
+        d_s[:, ls] = jnp.sum(ot_s[:, ls] * dot_s[:, ls].astype(F32), axis=0, keepdims=True) * rl
 
     def part_copy(msg, src, dst_ref, d, j, sem):
         return pltpu.make_async_remote_copy(
@@ -295,7 +304,7 @@
             merge_send(AT, 1, R_AT, dev_f)
 
     def bwd_body(t0, carry):
-        i = N_SLOT - 1 - t0
+        i = lax.rem(2 * N_SLOT - 2 - t0, N_SLOT)
         pl.when(here(i))(lambda: bwd_compute(i))
 
         @pl.when(jnp.logical_and(i == AO, e_bo))
@@ -316,7 +325,10 @@
 
     for t in range(NQ // TILE):
         ls = pl.ds(t * TILE, TILE)
+        o_s[ls, :] = (ot_s[:, ls] * l_s[:, ls]).T.astype(BF16)
         dq_s[ls, :] = (dqt_s[:, ls] * SCALE).T.astype(BF16)
+    o_out = pltpu.make_async_copy(o_s, o_hbm, lsem.at[4])
+    o_out.start()
     dq_out = pltpu.make_async_copy(dq_s, dq_hbm, lsem.at[5])
     dq_out.start()
 
@@ -358,8 +370,8 @@
         outs.append(c)
 
     up1 = jnp.logical_and(has_up, e1)
-    kv_sent = ((M_Y1, has_up), (M_Y2, up1), (M_AT, e1), (M_AO, e1), (M_A2, e1),
-               (M_BT, jnp.logical_or(x_g > x, e2)), (M_BO, jnp.logical_or(x_f > x, e2)), (M_B2, e_bo),
+    kv_sent = ((M_Y1, has_up), (M_Y2, up1), (M_AT, e1), (M_AO, e1), (M_A2, jnp.logical_and(e1, jnp.logical_or(x >= 2, has_up))),
+               (M_BT, jnp.logical_or(x_g > x, e2)), (M_BO, jnp.logical_or(x_f > x, e2)), (M_B2, jnp.logical_or(x < 2, has_up)),
                (M_P[PY1], e1), (M_P[PAT], e1), (M_P[PAO], e1), (M_P[PA2], e1), (M_P[PBT], e_bt), (M_P[PBO], e_bo),
                (M_P[PB2], e_b2), (M_P[PS], r_ps))
     part_sent = ((0, e1), (1, e1), (2, e1), (3, e1), (4, e_bt), (5, e_bo), (6, e_b2), (7, jnp.logical_or(core == 1, e2)),
@@ -411,6 +423,8 @@
                 pltpu.VMEM((NQ, HD), BF16),
                 pltpu.VMEM((NQ, HD), BF16),
                 pltpu.VMEM((2, CH, HD), BF16),
+                pltpu.VMEM((1, NQ), F32),
+                pltpu.VMEM((CH, NQ), BF16),
                 pltpu.SemaphoreType.DMA((8,)),
                 pltpu.SemaphoreType.DMA((16, 2)),
                 pltpu.SemaphoreType.DMA((N_SLOT, 2)),

time: 70.7 us -> 63.6 us (0.90)
  the two profiles are of different devices: /device:TPU:62 before, /device:TPU:88 now
where the time goes in v3:
time: 63.6 us; the launch traced here: 63.4 us
  Pallas kernels  58.6 us (92%)
  local copies, waits for them, and re-layouts  4.14 us (7%)
  between operations  0.65 us (1%)
    pallas_call x1, Pallas kernels, local_attn(): pl.pallas_call(kernel, out_shape=(jax.ShapeDtypeStruct((NQ, HD), BF16), j...  58.6 us
    unnamed x10, local copies, waits for them, and re-layouts  4.14 us

profile of v3, /device:TPU:88, one launch (start us, length us, event | category | flops | bytes accessed | tf_op | source)
XLA Modules:
  0.0 63.4 jit_solution(4515647728272613505)
XLA Ops:
  0.6 58.6 %swa_fwd_bwd.1 = (bf16[1024,128]{1,0:T(8,128)(2,1)}, bf16[1024,128]{1,0:T(8,128)(2,1)}, bf16[256,128]{1,0:T(8,128)(2,1)}, bf16[256,128]{1,0:T(8,128)(2,1)}) custom-call(bf16[1024,128]{1,0:T(8,128)(2,1)} %bitcast.8, bf16[256,128]{1,0:T(8,128)(2,1)} %bitcast.12, bf16[256,128]{1,0:T(8,128)(2,1)} %bitcast.13, bf16[1024,128]{1,0:T(8,128)(2,1)} %bitcast.9), custom_call_target="tpu_custom_call" | custom-call | tf_op jit(solution)/shard_map/swa_fwd_bwd/pallas_call | solution.py:400
  59.3 0.0 copy-start
  59.3 1.8 %copy.12 = bf16[1,256,4,128]{3,2,1,0:T(4,128)(2,1)} copy(bf16[1,256,4,128]{3,2,1,0:T(4,128)(2,1)} %bitcast.11) | data formatting | bytes 524288
  61.1 0.0 copy-done
  61.1 0.0 copy-start.2
  61.1 0.7 %copy.13 = bf16[1,256,4,128]{3,2,1,0:T(4,128)(2,1)} copy(bf16[1,256,4,128]{3,2,1,0:T(4,128)(2,1)S(1)} %bitcast.10) | data formatting | bytes 524288
  61.8 0.2 copy-done.2
  61.9 0.0 copy-start.1
  61.9 0.6 copy.14
  62.5 0.2 copy-done.1
  62.8 0.6 copy.15
Async XLA Ops:
  59.3 1.8 %copy-start = (bf16[1024,128]{1,0:T(8,128)(2,1)S(1)}, bf16[1024,128]{1,0:T(8,128)(2,1)}, u32[]{:S(2)}) copy-start(bf16[1024,128]{1,0:T(8,128)(2,1)} %get-tuple-element.9) | copy-start | bytes 786436
  61.1 0.9 %copy-start.2 = (bf16[256,128]{1,0:T(8,128)(2,1)S(1)}, bf16[256,128]{1,0:T(8,128)(2,1)}, u32[]{:S(2)}) copy-start(bf16[256,128]{1,0:T(8,128)(2,1)} %get-tuple-element.10) | copy-start | bytes 196612
  61.9 0.9 %copy-start.1 = (bf16[256,128]{1,0:T(8,128)(2,1)S(1)}, bf16[256,128]{1,0:T(8,128)(2,1)}, u32[]{:S(2)}) copy-start(bf16[256,128]{1,0:T(8,128)(2,1)} %get-tuple-element.11) | copy-start | bytes 196612

commit v4 on v3

--- a/solution.py
+++ b/solution.py
@@ -238,33 +238,46 @@
         l_s[:, ls] = rl
         d_s[:, ls] = jnp.sum(ot_s[:, ls] * dot_s[:, ls].astype(F32), axis=0, keepdims=True) * rl
 
-    def part_copy(msg, src, dst_ref, d, j, sem):
+    def part_copy(msg, src, dst_ref, d, q, sem):
         return pltpu.make_async_remote_copy(
-            src_ref=part.at[src, j], dst_ref=dst_ref, send_sem=bs.at[msg, j], recv_sem=br.at[sem, j],
+            src_ref=part.at[src, q], dst_ref=dst_ref, send_sem=bs.at[msg, q], recv_sem=br.at[sem, q],
             device_id=dev(d), device_id_type=pl.DeviceIdType.MESH)
 
-    R_A2, R_B2, R_AT, R_AO, R_BT, R_BO, R_Y2, R_YA = range(8)
+    R_DN, R_2, R_AT, R_AO, R_BT, R_BO, R_Y2, R_YA = range(8)
+    ORDER = (2, 3, 0, 1)
 
     def give(src, n):
-        for j in (1, 0):
-            part_copy(n, src, dr.at[n, j], partner, j, n).start()
-
-    def got(n, j):
-        part_copy(n, 0, dr.at[n, j], partner, j, n).wait_recv()
-
-    def send(src, n, d, j):
-        part_copy(8 + n, src, rx.at[n, j], d, j, 8 + n).start()
-
-    def recv(n, j):
-        part_copy(8 + n, 0, rx.at[n, j], partner, j, 8 + n).wait_recv()
+        for q in ORDER:
+            part_copy(n, src, dr.at[n, q], partner, q, n).start()
+
+    def add_dr(slot, n, q):
+        part_copy(n, 0, dr.at[n, q], partner, q, n).wait_recv()
+        part[slot, q] += dr[n, q]
+
+    def send(src, n, d, q):
+        part_copy(8 + n, src, rx.at[n, q], d, q, 8 + n).start()
+
+    def add_rx(slot, n, q):
+        part_copy(8 + n, 0, rx.at[n, q], partner, q, 8 + n).wait_recv()
+        part[slot, q] += rx[n, q]
 
     D_SLOT = {PY1: 0, PAT: 1, PAO: 2, PA2: 3, PBT: 4, PBO: 5, PB2: 6, PS: 7}
 
     def merge_send(slot, n_d, n_r, d):
-        for j in (1, 0):
-            got(n_d, j)
-            part[slot, j] += dr[n_d, j]
-            send(slot, n_r, d, j)
+        for q in ORDER:
+            add_dr(slot, n_d, q)
+            send(slot, n_r, d, q)
+
+    hi = (x >= 2).astype(jnp.int32)
+    low = x < 2
+    s_dn, n_dn = B2 + hi * (A2 - B2), 6 - hi * 3
+    s_x2, n_x2 = A2 + hi * (B2 - A2), 3 + hi * 3
+    e_dn = jnp.logical_or(jnp.logical_and(low, e2), jnp.logical_and(x >= 2, e1))
+    e_x2 = jnp.logical_or(x >= 2, e1)
+    r_dn = jnp.logical_and(has_up, e_x2)
+    r_x2 = jnp.logical_or(low, e1)
+
+    B_ORDER = (PBT, PBO, BT, BO, PB2, PA2, B2, A2, PAT, PAO, AT, AO, PS, Y2, PY1, Y1, OWN)
 
     def bwd_compute(i):
         kb = kv[i, 0]
@@ -279,49 +292,69 @@
             ds = (p * (dp_buf[i, :, ls] - d_s[:, ls])).astype(BF16)
             dk = dk + dot(ds, q_s[ls, :])
             dqt_s[:, ls] += dot(kt, ds)
-        part[i, 0] = dk * SCALE
-        part[i, 1] = dv
+        half = CH // 2
+        part[i, 0] = dk[:half] * SCALE
+        part[i, 1] = dk[half:] * SCALE
+        part[i, 2] = dv[:half]
+        part[i, 3] = dv[half:]
 
         for slot, n in D_SLOT.items():
             @pl.when(i == slot)
             def _(slot=slot, n=n):
                 give(slot, n)
 
-        @pl.when(i == B2)
-        def _():
-            merge_send(B2, 6, R_B2, dev_g)
-
-        @pl.when(i == BT)
-        def _():
-            merge_send(BT, 4, R_BT, dev_g)
-
-        @pl.when(i == A2)
-        def _():
-            merge_send(A2, 3, R_A2, dev_f)
-
         @pl.when(i == AT)
         def _():
             merge_send(AT, 1, R_AT, dev_f)
 
+        @pl.when(i == AO)
+        def _():
+            merge_send(AO, 2, R_AO, dev_g)
+
+        @pl.when(i == Y1)
+        def _():
+            for q in ORDER:
+                add_dr(Y1, 0, q)
+
     def bwd_body(t0, carry):
-        i = lax.rem(2 * N_SLOT - 2 - t0, N_SLOT)
+        i = jnp.int32(0)
+        for t, slot in enumerate(B_ORDER):
+            i = i + (t0 == t).astype(jnp.int32) * slot
         pl.when(here(i))(lambda: bwd_compute(i))
 
-        @pl.when(jnp.logical_and(i == AO, e_bo))
-        def _():
-            relay(BO, 5, R_B2, R_BO, dev_f)
+        @pl.when(i == PB2)
+        def _():
+            pl.when(e_bt)(lambda: merge_send(BT, 4, R_BT, dev_g))
+            pl.when(e_bo)(lambda: merge_send(BO, 5, R_BO, dev_f))
+
+        @pl.when(jnp.logical_and(i == PAO, e_dn))
+        def _():
+            merge_send(s_dn, n_dn, R_DN, down)
 
         return carry
 
-    def relay(slot, n_d, n_in, n_out, d):
-        for j in (1, 0):
-            got(n_d, j)
-            recv(n_in, j)
-            part[slot, j] += dr[n_d, j] + rx[n_in, j]
-            send(slot, n_out, d, j)
-
     lax.fori_loop(0, N_SLOT, bwd_body, 0)
-    pl.when(e1)(lambda: relay(AO, 2, R_A2, R_AO, dev_g))
+
+    def home_or_far(far):
+        return far.astype(jnp.int32) * Y2
+
+    r_bt = jnp.logical_or(x < x_g, e2)
+    r_bo = jnp.logical_or(x < x_f, e2)
+    r_ps = jnp.logical_or(core == 0, e2)
+    r_y2 = jnp.logical_and(has_up, e1)
+
+    for q in ORDER:
+        @pl.when(e_x2)
+        def _():
+            add_dr(s_x2, n_x2, q)
+            pl.when(r_dn)(lambda: add_rx(s_x2, R_DN, q))
+            send(s_x2, R_2, dev_2, q)
+
+    for q in ORDER:
+        pl.when(r_ps)(lambda: add_dr(core * Y2, 7, q))
+        pl.when(r_bt)(lambda: add_rx(home_or_far(x_g < x), R_BT, q))
+        pl.when(r_bo)(lambda: add_rx(home_or_far(x_f < x), R_BO, q))
+        pl.when(e2)(lambda: send(Y2, R_Y2, down, q))
 
     for t in range(NQ // TILE):
         ls = pl.ds(t * TILE, TILE)
@@ -332,39 +365,21 @@
     dq_out = pltpu.make_async_copy(dq_s, dq_hbm, lsem.at[5])
     dq_out.start()
 
-    def home_or_far(far):
-        return far.astype(jnp.int32) * Y2
-
-    def add_rx(slot, n, j):
-        recv(n, j)
-        part[slot, j] += rx[n, j]
-
-    r_bt = jnp.logical_or(x < x_g, e2)
-    r_bo = jnp.logical_or(x < x_f, e2)
-    r_ps = jnp.logical_or(core == 0, e2)
-    r_y2 = jnp.logical_and(has_up, e1)
-    for j in (1, 0):
-        @pl.when(r_ps)
-        def _():
-            got(7, j)
-            part[core * Y2, j] += dr[7, j]
-
-        pl.when(r_bt)(lambda: add_rx(home_or_far(x_g < x), R_BT, j))
-        pl.when(r_bo)(lambda: add_rx(home_or_far(x_f < x), R_BO, j))
-        pl.when(e2)(lambda: send(Y2, R_Y2, down, j))
-    for j in (1, 0):
+    for q in ORDER:
         @pl.when(e1)
         def _():
-            got(0, j)
-            part[Y1, j] += dr[0, j]
-            add_rx(Y1, R_AT, j)
-            add_rx(Y1, R_AO, j)
-            pl.when(has_up)(lambda: add_rx(Y1, R_Y2, j))
-            send(Y1, R_YA, down, j)
+            add_rx(Y1, R_AT, q)
+            add_rx(Y1, R_AO, q)
+            pl.when(has_up)(lambda: add_rx(Y1, R_Y2, q))
+
+    for q in ORDER:
+        pl.when(r_x2)(lambda: add_rx(hi * Y1, R_2, q))
+        pl.when(e1)(lambda: send(Y1, R_YA, down, q))
+    for q in ORDER:
+        pl.when(has_up)(lambda: add_rx(OWN, R_YA, q))
+        dkv_s[q // 2, pl.ds(q % 2 * (CH // 2), CH // 2), :] = part[OWN, q].astype(BF16)
     outs = []
     for j, hbm in ((1, dv_hbm), (0, dk_hbm)):
-        pl.when(has_up)(lambda: add_rx(OWN, R_YA, j))
-        dkv_s[j] = part[OWN, j].astype(BF16)
         c = pltpu.make_async_copy(dkv_s.at[j], hbm, lsem.at[6 + j])
         c.start()
         outs.append(c)
@@ -375,13 +390,14 @@
                (M_P[PY1], e1), (M_P[PAT], e1), (M_P[PAO], e1), (M_P[PA2], e1), (M_P[PBT], e_bt), (M_P[PBO], e_bo),
                (M_P[PB2], e_b2), (M_P[PS], r_ps))
     part_sent = ((0, e1), (1, e1), (2, e1), (3, e1), (4, e_bt), (5, e_bo), (6, e_b2), (7, jnp.logical_or(core == 1, e2)),
-                 (8 + R_A2, e1), (8 + R_B2, e_b2), (8 + R_AT, e1), (8 + R_AO, e1), (8 + R_BT, e_bt), (8 + R_BO, e_bo),
+                 (8 + R_DN, e_dn), (8 + R_2, e_x2), (8 + R_AT, e1), (8 + R_AO, e1), (8 + R_BT, e_bt), (8 + R_BO, e_bo),
                  (8 + R_Y2, e2), (8 + R_YA, e1))
     for j in range(2):
         for msg, e in kv_sent:
             pl.when(e)(lambda: kv_copy(msg, 0, 0, partner, j).wait_send())
+    for q in range(4):
         for msg, e in part_sent:
-            pl.when(e)(lambda: part_copy(msg, 0, dr.at[0, j], partner, j, 0).wait_send())
+            pl.when(e)(lambda: part_copy(msg, 0, dr.at[0, q], partner, q, 0).wait_send())
     o_out.wait()
     dq_out.wait()
     for c in outs:
@@ -417,9 +433,9 @@
                 pltpu.VMEM((1, NQ), F32),
                 pltpu.VMEM((HD, NQ), F32),
                 pltpu.VMEM((HD, NQ), F32),
-                pltpu.VMEM((N_SLOT, 2, CH, HD), F32),
-                pltpu.VMEM((8, 2, CH, HD), F32),
-                pltpu.VMEM((8, 2, CH, HD), F32),
+                pltpu.VMEM((N_SLOT, 4, CH // 2, HD), F32),
+                pltpu.VMEM((8, 4, CH // 2, HD), F32),
+                pltpu.VMEM((8, 4, CH // 2, HD), F32),
                 pltpu.VMEM((NQ, HD), BF16),
                 pltpu.VMEM((NQ, HD), BF16),
                 pltpu.VMEM((2, CH, HD), BF16),
@@ -428,8 +444,8 @@
                 pltpu.SemaphoreType.DMA((8,)),
                 pltpu.SemaphoreType.DMA((16, 2)),
                 pltpu.SemaphoreType.DMA((N_SLOT, 2)),
-                pltpu.SemaphoreType.DMA((16, 2)),
-                pltpu.SemaphoreType.DMA((16, 2)),
+                pltpu.SemaphoreType.DMA((16, 4)),
+                pltpu.SemaphoreType.DMA((16, 4)),
             ],
             compiler_params=pltpu.CompilerParams(
                 collective_id=0, has_side_effects=True, vmem_limit_bytes=63 * 1024 * 1024),

time: 63.6 us -> 62.7 us (0.986)
  the two profiles are of different devices: /device:TPU:88 before, /device:TPU:16 now
where the time goes in v4:
time: 62.7 us; the launch traced here: 62.1 us
  Pallas kernels  57.3 us (91%)
  local copies, waits for them, and re-layouts  4.14 us (7%)
  between operations  0.65 us (1%)
    pallas_call x1, Pallas kernels, local_attn(): pl.pallas_call(kernel, out_shape=(jax.ShapeDtypeStruct((NQ, HD), BF16), j...  57.3 us
    unnamed x10, local copies, waits for them, and re-layouts  4.14 us

profile of v4, /device:TPU:16, one launch (start us, length us, event | category | flops | bytes accessed | tf_op | source)
XLA Modules:
  0.0 62.1 jit_solution(3174230663983595241)
XLA Ops:
  0.6 57.3 %swa_fwd_bwd.1 = (bf16[1024,128]{1,0:T(8,128)(2,1)}, bf16[1024,128]{1,0:T(8,128)(2,1)}, bf16[256,128]{1,0:T(8,128)(2,1)}, bf16[256,128]{1,0:T(8,128)(2,1)}) custom-call(bf16[1024,128]{1,0:T(8,128)(2,1)} %bitcast.8, bf16[256,128]{1,0:T(8,128)(2,1)} %bitcast.12, bf16[256,128]{1,0:T(8,128)(2,1)} %bitcast.13, bf16[1024,128]{1,0:T(8,128)(2,1)} %bitcast.9), custom_call_target="tpu_custom_call" | custom-call | tf_op jit(solution)/shard_map/swa_fwd_bwd/pallas_call | solution.py:416
  58.0 0.0 copy-start
  58.0 1.8 %copy.12 = bf16[1,256,4,128]{3,2,1,0:T(4,128)(2,1)} copy(bf16[1,256,4,128]{3,2,1,0:T(4,128)(2,1)} %bitcast.11) | data formatting | bytes 524288
  59.8 0.0 copy-done
  59.8 0.0 copy-start.2
  59.8 0.7 %copy.13 = bf16[1,256,4,128]{3,2,1,0:T(4,128)(2,1)} copy(bf16[1,256,4,128]{3,2,1,0:T(4,128)(2,1)S(1)} %bitcast.10) | data formatting | bytes 524288
  60.5 0.2 copy-done.2
  60.6 0.0 copy-start.1
  60.6 0.6 %copy.14 = bf16[1,256,1,128]{3,1,2,0:T(8,128)(2,1)} copy(bf16[1,256,1,128]{3,1,2,0:T(8,128)(2,1)S(1)} %bitcast.15) | data formatting | bytes 131072
  61.3 0.2 copy-done.1
  61.5 0.6 %copy.15 = bf16[1,256,1,128]{3,1,2,0:T(8,128)(2,1)} copy(bf16[1,256,1,128]{3,1,2,0:T(8,128)(2,1)S(1)} %bitcast.14) | data formatting | bytes 131072
Async XLA Ops:
  58.0 1.8 %copy-start = (bf16[1024,128]{1,0:T(8,128)(2,1)S(1)}, bf16[1024,128]{1,0:T(8,128)(2,1)}, u32[]{:S(2)}) copy-start(bf16[1024,128]{1,0:T(8,128)(2,1)} %get-tuple-element.9) | copy-start | bytes 786436
  59.8 0.9 %copy-start.2 = (bf16[256,128]{1,0:T(8,128)(2,1)S(1)}, bf16[256,128]{1,0:T(8,128)(2,1)}, u32[]{:S(2)}) copy-start(bf16[256,128]{1,0:T(8,128)(2,1)} %get-tuple-element.10) | copy-start | bytes 196612
  60.6 0.9 %copy-start.1 = (bf16[256,128]{1,0:T(8,128)(2,1)S(1)}, bf16[256,128]{1,0:T(8,128)(2,1)}, u32[]{:S(2)}) copy-start(bf16[256,128]{1,0:T(8,128)(2,1)} %get-tuple-element.11) | copy-start | bytes 196612

commit v5 on v4

--- a/solution.py
+++ b/solution.py
@@ -275,9 +275,8 @@
     e_dn = jnp.logical_or(jnp.logical_and(low, e2), jnp.logical_and(x >= 2, e1))
     e_x2 = jnp.logical_or(x >= 2, e1)
     r_dn = jnp.logical_and(has_up, e_x2)
-    r_x2 = jnp.logical_or(low, e1)
-
-    B_ORDER = (PBT, PBO, BT, BO, PB2, PA2, B2, A2, PAT, PAO, AT, AO, PS, Y2, PY1, Y1, OWN)
+
+    B_ORDER = (PBT, PBO, PB2, PA2, BT, BO, B2, A2, PAT, PAO, PS, Y2, AT, AO, PY1, Y1, OWN)
 
     def bwd_compute(i):
         kb = kv[i, 0]
@@ -303,6 +302,14 @@
             def _(slot=slot, n=n):
                 give(slot, n)
 
+        @pl.when(i == BT)
+        def _():
+            merge_send(BT, 4, R_BT, dev_g)
+
+        @pl.when(i == BO)
+        def _():
+            merge_send(BO, 5, R_BO, dev_f)
+
         @pl.when(i == AT)
         def _():
             merge_send(AT, 1, R_AT, dev_f)
@@ -310,11 +317,6 @@
         @pl.when(i == AO)
         def _():
             merge_send(AO, 2, R_AO, dev_g)
-
-        @pl.when(i == Y1)
-        def _():
-            for q in ORDER:
-                add_dr(Y1, 0, q)
 
     def bwd_body(t0, carry):
         i = jnp.int32(0)
@@ -322,12 +324,7 @@
             i = i + (t0 == t).astype(jnp.int32) * slot
         pl.when(here(i))(lambda: bwd_compute(i))
 
-        @pl.when(i == PB2)
-        def _():
-            pl.when(e_bt)(lambda: merge_send(BT, 4, R_BT, dev_g))
-            pl.when(e_bo)(lambda: merge_send(BO, 5, R_BO, dev_f))
-
-        @pl.when(jnp.logical_and(i == PAO, e_dn))
+        @pl.when(jnp.logical_and(i == A2, e_dn))
         def _():
             merge_send(s_dn, n_dn, R_DN, down)
 
@@ -341,16 +338,15 @@
     r_bt = jnp.logical_or(x < x_g, e2)
     r_bo = jnp.logical_or(x < x_f, e2)
     r_ps = jnp.logical_or(core == 0, e2)
-    r_y2 = jnp.logical_and(has_up, e1)
-
-    for q in ORDER:
-        @pl.when(e_x2)
+
+    def cross(q, e):
+        @pl.when(e)
         def _():
             add_dr(s_x2, n_x2, q)
             pl.when(r_dn)(lambda: add_rx(s_x2, R_DN, q))
             send(s_x2, R_2, dev_2, q)
 
-    for q in ORDER:
+    def far(q):
         pl.when(r_ps)(lambda: add_dr(core * Y2, 7, q))
         pl.when(r_bt)(lambda: add_rx(home_or_far(x_g < x), R_BT, q))
         pl.when(r_bo)(lambda: add_rx(home_or_far(x_f < x), R_BO, q))
@@ -365,17 +361,24 @@
     dq_out = pltpu.make_async_copy(dq_s, dq_hbm, lsem.at[5])
     dq_out.start()
 
+    for pair in ((2, 3), (0, 1)):
+        for q in pair:
+            far(q)
+        for q in pair:
+            cross(q, jnp.logical_and(low, e1))
+    for q in ORDER:
+        cross(q, x >= 2)
     for q in ORDER:
         @pl.when(e1)
         def _():
+            add_dr(Y1, 0, q)
             add_rx(Y1, R_AT, q)
             add_rx(Y1, R_AO, q)
             pl.when(has_up)(lambda: add_rx(Y1, R_Y2, q))
-
+            pl.when(x >= 2)(lambda: add_rx(Y1, R_2, q))
+            send(Y1, R_YA, down, q)
     for q in ORDER:
-        pl.when(r_x2)(lambda: add_rx(hi * Y1, R_2, q))
-        pl.when(e1)(lambda: send(Y1, R_YA, down, q))
-    for q in ORDER:
+        pl.when(low)(lambda: add_rx(OWN, R_2, q))
         pl.when(has_up)(lambda: add_rx(OWN, R_YA, q))
         dkv_s[q // 2, pl.ds(q % 2 * (CH // 2), CH // 2), :] = part[OWN, q].astype(BF16)
     outs = []
@@ -400,6 +403,19 @@
             pl.when(e)(lambda: part_copy(msg, 0, dr.at[0, q], partner, q, 0).wait_send())
     o_out.wait()
     dq_out.wait()
+    for c in outs:
+        c.wait()
+
+
+def emit_kernel(*refs):
+    src, dst, buf, sem_in, sem_out = refs[:4], refs[4:8], refs[8:12], refs[12], refs[13]
+    ins = [pltpu.make_async_copy(src[n], buf[n], sem_in.at[n]) for n in range(4)]
+    outs = [pltpu.make_async_copy(buf[n], dst[n], sem_out.at[n]) for n in range(4)]
+    for c in ins:
+        c.start()
+    for n in range(4):
+        ins[n].wait()
+        outs[n].start()
     for c in outs:
         c.wait()
 
@@ -451,6 +467,15 @@
                 collective_id=0, has_side_effects=True, vmem_limit_bytes=63 * 1024 * 1024),
             name='swa_fwd_bwd',
         )(q, k, v, do)
+        anyspec4 = [anyspec] * 4
+        o, dq, dk, dv = pl.pallas_call(
+            emit_kernel,
+            out_shape=tuple(jax.ShapeDtypeStruct(a.shape, BF16) for a in (o, dq, dk, dv)),
+            in_specs=anyspec4,
+            out_specs=anyspec4,
+            scratch_shapes=[pltpu.VMEM(a.shape, BF16) for a in (o, dq, dk, dv)] + [pltpu.SemaphoreType.DMA((4,))] * 2,
+            name='emit',
+        )(o, dq, dk, dv)
         return o.reshape(q_loc.shape), dq.reshape(q_loc.shape), dk.reshape(k_loc.shape), dv.reshape(k_loc.shape)
 
     return jax.shard_map(local_attn, mesh=mesh, in_specs=(seq_spec,) * 4, out_specs=(seq_spec,) * 4, check_vma=False)

time: 62.7 us -> 56.7 us (0.904)
  local copies, waits for them, and re-layouts: 4.14 us -> 0 us
  Pallas kernels: 57.3 us -> 55.6 us
    unnamed x10 -> x0, local copies, waits for them, and re-layouts: 4.14 us -> none
    pallas_call x1, Pallas kernels: 57.3 us -> 53.8 us  [local_attn(): pl.pallas_call(kernel, out_shape=(jax.ShapeDtypeStruct((NQ, HD), BF16), j...]
    pallas_call x0 -> x1, Pallas kernels: none -> 1.84 us  [local_attn(): pl.pallas_call(emit_kernel, out_shape=tuple((jax.ShapeDtypeStruct(a.shape...]
where the time goes in v5:
time: 56.7 us; the launch traced here: 56.3 us
  Pallas kernels  55.6 us (98%)
  between operations  0.64 us (1%)
    pallas_call x1, Pallas kernels, local_attn(): pl.pallas_call(kernel, out_shape=(jax.ShapeDtypeStruct((NQ, HD), BF16), j...  53.8 us
    pallas_call x1, Pallas kernels, local_attn(): pl.pallas_call(emit_kernel, out_shape=tuple((jax.ShapeDtypeStruct(a.shape...  1.84 us

profile of v5, /device:TPU:16, one launch (start us, length us, event | category | flops | bytes accessed | tf_op | source)
XLA Modules:
  0.0 56.3 jit_solution(17492414936109766822)
XLA Ops:
  0.6 53.8 %swa_fwd_bwd.1 = (bf16[1024,128]{1,0:T(8,128)(2,1)}, bf16[1024,128]{1,0:T(8,128)(2,1)}, bf16[256,128]{1,0:T(8,128)(2,1)}, bf16[256,128]{1,0:T(8,128)(2,1)}) custom-call(bf16[1024,128]{1,0:T(8,128)(2,1)} %bitcast.8, bf16[256,128]{1,0:T(8,128)(2,1)} %bitcast.10, bf16[256,128]{1,0:T(8,128)(2,1)} %bitcast.11, bf16[1024,128]{1,0:T(8,128)(2,1)} %bitcast.9), custom_call_target="tpu_custom_call" | custom-call | tf_op jit(solution)/shard_map/swa_fwd_bwd/pallas_call | solution.py:432
  54.4 1.8 %emit.1 = (bf16[1024,128]{1,0:T(8,128)(2,1)}, bf16[1024,128]{1,0:T(8,128)(2,1)}, bf16[256,128]{1,0:T(8,128)(2,1)}, bf16[256,128]{1,0:T(8,128)(2,1)}) custom-call(bf16[1024,128]{1,0:T(8,128)(2,1)} %get-tuple-element.12.refs_0_, bf16[1024,128]{1,0:T(8,128)(2,1)} %get-tuple-element.13.refs_1_, bf16[256,128]{1,0:T(8,128)(2,1)} %get-tuple-element.14.refs_2_, ...), custom_call_target="tpu_custom_call" | custom-call | tf_op jit(solution)/shard_map/emit/pallas_call | solution.py:471
